TPU v7x, 128 devices: a whole 4x4x4 slice. The times are simulated.
128 devices in a mesh: ep: 32 (over y, z, core), dp: 4 (over x).
Axes of the slice: x: 4, y: 4, z: 4, core: 2. Of those that a mesh axis runs over, the one named last changes fastest.
Arguments:
- tokens: bfloat16 [24576, 2880], P(('ep', 'dp')), may hold values from -64 to 64
- out_grad: bfloat16 [24576, 2880], P(('ep', 'dp')), may hold values from -6 to 6
- indices: int32 [24576, 4], P(('ep', 'dp')), may hold values from 0 to 127, as said below
- expert_rows: bfloat16 [4, 128, 32, 9, 2880], P('dp', 'ep'), may hold values from -0.111328125 to 0.111328125
- router_weight: bfloat16 [2880, 128], replicated, may hold values from -1 to 1
- router_bias: float32 [128], replicated, may hold values from -3 to 3
- balance_scale: float32 [1], replicated, may hold values from 64 to 256
Outputs:
- token_grad: bfloat16 [24576, 2880], P(('ep', 'dp'))
- weight_grad: float32 [2880, 128], P('dp', 'ep')
- balance_loss: float32 [1], replicated
Inputs may be any that keep to these rules, and one draw needn't show every extreme that they name: `indices`: each row names 4 different experts. Within the 192 rows of one device no expert is named by more than 9 rows, and some expert is named by exactly 9 rows. Within the rows of one device the 4 experts of one ep index (experts j * 4 to j * 4 + 3) are named by at most 27 rows together, and those of some ep index by exactly 27. Every expert is named by some row of every device.
All inputs are finite; a program needn't handle non-finite values.
Results may differ from a plain program's by a relative error of at most 0.0014.
The roundings to bfloat16 on the way count: a program that leaves them out, or rounds other values in their place, can miss the bound.
Values may be sent and summed in bfloat16 or wider, within the bound.
A program may use at most 128 MiB of HBM per device.

v0:
```python
import functools
import math

import jax
import jax.numpy as jnp
from jax import lax
from jax.sharding import Mesh
from jax.sharding import PartitionSpec as P

EP = ("ep_0", "ep_1", "ep_2")
EP_DP = ("ep_0", "ep_1", "ep_2", "dp")


def by_axis(shard, axes):
    return functools.reduce(lax.psum, axes, shard)


def split_up(shard, dim, count):
    before, after = (shard.shape[:dim], shard.shape[dim + 1 :])
    return jnp.moveaxis(shard.reshape(*before, count, -1, *after), dim, 0)


def cut_rows(length, count):
    unit = 8 if length >= 8 * count else 1
    return [length // unit * k // count * unit for k in range(1, count)]


def in_order(pieces, dim):
    pieces = jnp.moveaxis(pieces, 0, dim)
    dims = pieces.shape
    return pieces.reshape(*dims[:dim], dims[dim] * dims[dim + 1], *dims[dim + 2 :])


def several_exchanges(shard, axis, pieces, split_dim, concat_dim):
    blocks = split_up(shard, split_dim, lax.axis_size(axis))
    widest = max(range(1, max(2, blocks.ndim - 1)), key=lambda d: blocks.shape[d])
    gathered = []
    for share in jnp.split(blocks, cut_rows(blocks.shape[widest], pieces), axis=widest):
        if share.size:
            gathered.append(lax.all_to_all(share, axis, split_axis=0, concat_axis=0, tiled=True))
    return in_order(jnp.concatenate(gathered, axis=widest), concat_dim)


def summed_on_arrival(shard, axis, dim):
    pieces = split_up(shard, dim, lax.axis_size(axis))
    arrived = lax.all_to_all(pieces, axis, split_axis=0, concat_axis=0, tiled=True)
    return arrived.sum(axis=0)


def on_device(tokens, out_grad, indices, expert_rows, router_weight, router_bias, balance_scale):
    tok_dev = tokens.shape[0]
    chosen = indices.shape[1]
    width = tokens.shape[1]
    experts = router_weight.shape[1]
    capacity = expert_rows.shape[3]
    ep_size = lax.axis_size(EP)
    dp_size = lax.axis_size("dp")
    token_total = tok_dev * ep_size * dp_size
    expert_ids = jnp.arange(experts, dtype=jnp.int32)
    onehot = (indices[:, :, None] == expert_ids[None, None, :]).astype(jnp.float32)
    named_by = jnp.sum(onehot, axis=1)
    local_counts = jnp.sum(named_by, axis=0)
    logits = jnp.dot(tokens, router_weight, preferred_element_type=jnp.float32) + router_bias
    probability = jax.nn.softmax(logits, axis=-1)
    counts, prob_sums = (by_axis(local_counts, EP_DP), by_axis(jnp.sum(probability, axis=0), EP_DP))
    share_of = counts / (token_total * chosen)
    balance_loss = (experts * jnp.sum(share_of * (prob_sums / token_total))).reshape(1)
    row_ids = jnp.arange(tok_dev, dtype=jnp.int32)
    lower_mask = (row_ids[:, None] > row_ids[None, :]).astype(jnp.bfloat16)
    before = jnp.dot(lower_mask, named_by.astype(jnp.bfloat16), preferred_element_type=jnp.float32)
    slot_index = jnp.sum(onehot * before[:, None, :], axis=2).astype(jnp.int32)
    returned = several_exchanges(expert_rows, EP, 2, 2, 1)
    flat_rows = returned.reshape(experts * capacity, width)
    row_index = indices * capacity + slot_index
    picked = jnp.take(flat_rows, row_index, axis=0)
    pair_dots = jnp.einsum("td,tkd->tk", out_grad, picked, preferred_element_type=jnp.float32)
    chosen_logits = jnp.take_along_axis(logits, indices, axis=1)
    mix_weight = jax.nn.softmax(chosen_logits, axis=-1)
    sel_grad = mix_weight * (pair_dots - jnp.sum(mix_weight * pair_dots, axis=1, keepdims=True))
    balance_push = balance_scale[0] * experts * share_of
    spread = probability * (
        balance_push[None, :] - jnp.sum(probability * balance_push[None, :], axis=1, keepdims=True)
    )
    logit_grad = (spread + jnp.sum(onehot * sel_grad[:, :, None], axis=1)).astype(jnp.bfloat16)
    token_grad = lax.dot_general(
        logit_grad, router_weight, (((1,), (1,)), ((), ())), preferred_element_type=jnp.float32
    ).astype(jnp.bfloat16)
    summed = summed_on_arrival(
        lax.dot_general(
            tokens, logit_grad, (((0,), (0,)), ((), ())), preferred_element_type=jnp.float32
        ),
        "dp",
        0,
    )
    summed = summed_on_arrival(summed, EP, 1)
    weight_grad = summed / math.sqrt(token_total)
    return (token_grad, weight_grad, balance_loss)


def solution(mesh):
    torus = Mesh(mesh.devices.reshape(4, 4, 2, mesh.shape["dp"]), ("ep_0", "ep_1", "ep_2", "dp"))
    return jax.shard_map(
        on_device,
        mesh=torus,
        in_specs=(
            P(EP_DP, None),
            P(EP_DP, None),
            P(EP_DP, None),
            P("dp", EP, None, None, None),
            P(),
            P(),
            P(),
        ),
        out_specs=(P(EP_DP, None), P("dp", EP), P()),
        check_vma=False,
    )
```

profile of v0, /device:TPU:1, one launch (start us, length us, event | category | flops | bytes accessed | tf_op | source)
XLA Modules:
  0.0 265.6 jit_solution(17196545560820542895)
XLA Ops:
  0.6 10.7 %copy.75 = bf16[1,4,32,9,2880]{4,3,1,2,0:T(8,128)(2,1)} copy(bf16[1,4,32,9,2880]{4,2,3,1,0:T(8,128)(2,1)} %param.10) | data formatting | bytes 13271040 | tf_op args[3]
  11.3 5.1 %split.8 = bf16[32,1,4,1,4,2880]{5,4,2,3,1,0:T(4,128)(2,1)} slice(bf16[32,1,4,1,9,2880]{5,4,2,3,1,0:T(8,128)(2,1)} %bitcast.35), slice={[0:32], [0:1], [0:4], [0:1], [0:4], [0:2880]} | slice | bytes 5898240 | tf_op jit(solution)/shard_map/split | solution.py:38
  16.4 9.6 %all-to-all-start = ((bf16[32,1,4,1,4,2880]{5,4,2,3,1,0:T(4,128)(2,1)}), bf16[32,1,4,1,4,2880]{5,4,2,3,1,0:T(4,128)(2,1)}, u32[]{:S(2)}, u32[]{:S(2)}) async-start(bf16[32,1,4,1,4,2880]{5,4,2,3,1,0:T(4,128)(2,1)} %split.8), calls=%async_computation | async-start | bytes 6029312 | tf_op jit(solution)/shard_map/all_to_all | solution.py:40
  26.0 6.2 %split.9 = bf16[32,1,4,1,5,2880]{5,4,2,3,1,0:T(8,128)(2,1)S(1)} slice(bf16[32,1,4,1,9,2880]{5,4,2,3,1,0:T(8,128)(2,1)} %bitcast.36), slice={[0:32], [0:1], [0:4], [0:1], [4:9], [0:2880]} | slice | bytes 7372800 | tf_op jit(solution)/shard_map/split | solution.py:38
  32.2 3.4 %copy.65 = bf16[32,1,4,1,5,2880]{5,2,4,3,1,0:T(4,128)(2,1)} copy(bf16[32,1,4,1,5,2880]{5,4,2,3,1,0:T(8,128)(2,1)S(1)} %split.9) | data formatting | bytes 7372800 | tf_op jit(solution)/shard_map/split | solution.py:38
  35.7 28.6 %all-to-all-done = bf16[32,1,4,1,4,2880]{5,4,2,3,1,0:T(4,128)(2,1)} async-done(((bf16[32,1,4,1,4,2880]{5,4,2,3,1,0:T(4,128)(2,1)}), bf16[32,1,4,1,4,2880]{5,4,2,3,1,0:T(4,128)(2,1)}, u32[]{:S(2)}, u32[]{:S(2)}) %all-to-all-start) | async-done | bytes 2949152 | tf_op jit(solution)/shard_map/all_to_all | solution.py:40
  64.3 5.2 %all-to-all-start.1 = ((bf16[32,1,4,1,5,2880]{5,2,4,3,1,0:T(4,128)(2,1)}), bf16[32,1,4,1,5,2880]{5,2,4,3,1,0:T(4,128)(2,1)}, u32[]{:S(2)}, u32[]{:S(2)}) async-start(bf16[32,1,4,1,5,2880]{5,2,4,3,1,0:T(4,128)(2,1)} %copy.65), calls=%async_computation.1 | async-start | bytes 7536640 | tf_op jit(solution)/shard_map/all_to_all | solution.py:40
  70.2 0.2 convert_reduce_fusion
  70.4 0.1 fusion.5
  70.5 0.4 convert_reduce_fusion.1
  70.9 0.2 copy.63
  71.1 0.1 copy.61
  71.2 0.1 reshape.58
  71.4 0.1 copy.68
  71.5 0.1 reshape.52
  71.6 0.6 fusion.17
  72.2 4.9 %gather_fusion.1 = f32[768]{0:T(1024)S(1)} fusion(f32[192,128]{1,0:T(8,128)S(1)} %get-tuple-element.13, s32[768]{0:T(1024)S(1)} %reshape.58), kind=kCustom, calls=%fused_computation.1 | custom fusion | bytes 12288 | tf_op jit(solution)/shard_map/jit(take_along_axis)/gather | solution.py:77
  77.1 0.1 reshape.61
  77.3 40.4 %psum.56 = f32[128]{0:T(128)S(1)} all-reduce(f32[128]{0:T(128)S(1)} %get-tuple-element.5), channel_id=1, replica_groups=mesh['ep_0'=4,'ep_1'=4,'ep_2'=2,'dp'=4] {'ep_0'}, use_global_device_ids=true, to_apply=%region_3.0 | all-reduce | flops 128 | bytes 1024 | tf_op jit(solution)/shard_map/psum | solution.py:15
  117.7 7.5 %psum.57 = f32[128]{0:T(128)S(1)} all-reduce(f32[128]{0:T(128)S(1)} %psum.56), channel_id=1, replica_groups=mesh['ep_0'=4,'ep_1'=4,'ep_2'=2,'dp'=4] {'ep_1'}, use_global_device_ids=true, to_apply=%region_4.0 | all-reduce | flops 128 | bytes 1024 | tf_op jit(solution)/shard_map/psum | solution.py:15
  125.3 5.9 %psum.58 = f32[128]{0:T(128)S(1)} all-reduce(f32[128]{0:T(128)S(1)} %psum.57), channel_id=1, replica_groups=mesh['ep_0'=4,'ep_1'=4,'ep_2'=2,'dp'=4] {'ep_2'}, use_global_device_ids=true, to_apply=%region_5.0 | all-reduce | flops 128 | bytes 1024 | tf_op jit(solution)/shard_map/psum | solution.py:15
  131.2 8.6 %psum.59 = f32[128]{0:T(128)S(1)} all-reduce(f32[128]{0:T(128)S(1)} %psum.58), channel_id=1, replica_groups=mesh['ep_0'=4,'ep_1'=4,'ep_2'=2,'dp'=4] {'dp'}, use_global_device_ids=true, to_apply=%region_6.0 | all-reduce | flops 128 | bytes 1024 | tf_op jit(solution)/shard_map/psum | solution.py:15
  139.9 0.2 fusion.7
  140.1 0.2 fusion.14
  140.3 4.7 %copy.66 = bf16[32,1,4,1,4,2880]{5,2,4,3,1,0:T(4,128)(2,1)} copy(bf16[32,1,4,1,4,2880]{5,4,2,3,1,0:T(4,128)(2,1)} %all-to-all-done) | data formatting | bytes 5898240 | tf_op jit(solution)/shard_map/all_to_all | solution.py:40
  145.0 10.2 %pad_maximum_fusion = bf16[32,1,4,1,9,2880]{5,2,4,3,1,0:T(4,128)(2,1)} fusion(bf16[32,1,4,1,5,2880]{5,2,4,3,1,0:T(4,128)(2,1)} %all-to-all-done.1, bf16[32,1,4,1,4,2880]{5,2,4,3,1,0:T(4,128)(2,1)} %copy.66), kind=kLoop, calls=%fused_computation.3 | loop fusion | flops 3317760 | bytes 13271040 | tf_op jit(solution)/shard_map/concatenate | solution.py:41
  155.2 9.6 %copy.67 = bf16[32,1,4,1,9,2880]{5,4,2,0,3,1:T(8,128)(2,1)} copy(bf16[32,1,4,1,9,2880]{5,2,4,3,1,0:T(4,128)(2,1)} %pad_maximum_fusion) | data formatting | bytes 13271040 | tf_op jit(solution)/shard_map/concatenate | solution.py:41
  164.8 13.9 %reshape_reshape_transpose.3 = bf16[1152,2880]{1,0:T(8,128)(2,1)} reshape(bf16[32,1,4,1,9,2880]{5,4,2,0,3,1:T(8,128)(2,1)} %copy.67) | data formatting | bytes 13271040 | tf_op jit(solution)/shard_map/reshape;reshape;transpose | solution.py:73
  178.7 13.1 %gather_fusion = bf16[768,2880]{1,0:T(8,128)(2,1)} fusion(bf16[1152,2880]{1,0:T(8,128)(2,1)} %reshape_reshape_transpose.3, s32[1024]{0:T(1024)S(1)} %pad_clamp_fusion), kind=kCustom, calls=%fused_computation | custom fusion | bytes 8850432 | tf_op jit(solution)/shard_map/jit(_take)/gather | solution.py:75
  191.8 7.1 %reshape.51 = bf16[192,4,2880]{2,1,0:T(4,128)(2,1)} reshape(bf16[768,2880]{1,0:T(8,128)(2,1)} %gather_fusion) | data formatting | bytes 8847360 | tf_op jit(solution)/shard_map/jit(_take)/gather | solution.py:75
  198.9 9.4 %fusion = f32[192,1,4]{2,1,0:T(1,128)S(1)} fusion(bf16[192,4,2880]{2,1,0:T(4,128)(2,1)} %reshape.51, pred[192,4]{1,0:T(8,128)(4,1)S(1)} %copy.63, bf16[192,2880,1]{1,0,2:T(8,128)(2,1)S(1)} %bitcast.34), kind=kOutput, calls=%fused_computation.4 | convolution fusion | flops 6635520 | bytes 5533440 | tf_op jit(solution)/shard_map/td,tkd->tk/dot_general | solution.py:76
  208.3 0.1 copy.71
  208.5 0.3 select_reduce_fusion
  208.7 0.1 add_convert_fusion
  208.8 1.8 fusion.18
  210.7 3.6 %all-to-all-start.2 = ((f32[4,720,128]{2,1,0:T(8,128)}), f32[4,720,128]{2,1,0:T(8,128)S(1)}, u32[]{:S(2)}, u32[]{:S(2)}) async-start(f32[4,720,128]{2,1,0:T(8,128)} %bitcast.37), calls=%async_computation.2 | async-start | bytes 2949120 | tf_op jit(solution)/shard_map/all_to_all | solution.py:46
  214.2 6.0 %psum.60 = f32[128]{0:T(128)S(1)} all-reduce(f32[128]{0:T(128)S(1)} %get-tuple-element.3), channel_id=1, replica_groups=mesh['ep_0'=4,'ep_1'=4,'ep_2'=2,'dp'=4] {'ep_0'}, use_global_device_ids=true, to_apply=%region_17.18 | all-reduce | flops 128 | bytes 1024 | tf_op jit(solution)/shard_map/psum | solution.py:15
  220.3 8.0 %psum.61 = f32[128]{0:T(128)S(1)} all-reduce(f32[128]{0:T(128)S(1)} %psum.60), channel_id=1, replica_groups=mesh['ep_0'=4,'ep_1'=4,'ep_2'=2,'dp'=4] {'ep_1'}, use_global_device_ids=true, to_apply=%region_18.19 | all-reduce | flops 128 | bytes 1024 | tf_op jit(solution)/shard_map/psum | solution.py:15
  228.2 7.6 %psum.62 = f32[128]{0:T(128)S(1)} all-reduce(f32[128]{0:T(128)S(1)} %psum.61), channel_id=1, replica_groups=mesh['ep_0'=4,'ep_1'=4,'ep_2'=2,'dp'=4] {'ep_2'}, use_global_device_ids=true, to_apply=%region_19.20 | all-reduce | flops 128 | bytes 1024 | tf_op jit(solution)/shard_map/psum | solution.py:15
  235.8 8.8 %psum.63 = f32[128]{0:T(128)S(1)} all-reduce(f32[128]{0:T(128)S(1)} %psum.62), channel_id=1, replica_groups=mesh['ep_0'=4,'ep_1'=4,'ep_2'=2,'dp'=4] {'dp'}, use_global_device_ids=true, to_apply=%region_20.21 | all-reduce | flops 128 | bytes 1024 | tf_op jit(solution)/shard_map/psum | solution.py:15
  244.7 0.8 reduce_sum.116
  245.5 1.1 copy.69
  246.7 0.8 reshape.48
  247.5 5.9 %all-to-all-start.3 = ((f32[32,720,4]{1,2,0:T(4,128)}), f32[32,720,4]{1,2,0:T(4,128)S(1)}, u32[]{:S(2)}, u32[]{:S(2)}) async-start(f32[32,720,4]{1,2,0:T(4,128)} %bitcast.9), calls=%async_computation.3 | async-start | bytes 786432 | tf_op jit(solution)/shard_map/all_to_all | solution.py:46
  253.4 0.6 multiply_reduce_fusion.1
  254.7 1.5 convolution_convert_fusion
  256.1 7.7 %all-to-all-done.3 = f32[32,720,4]{1,2,0:T(4,128)S(1)} async-done(((f32[32,720,4]{1,2,0:T(4,128)}), f32[32,720,4]{1,2,0:T(4,128)S(1)}, u32[]{:S(2)}, u32[]{:S(2)}) %all-to-all-start.3) | async-done | bytes 368672 | tf_op jit(solution)/shard_map/all_to_all | solution.py:46
  263.9 0.6 broadcast_multiply_fusion
  (22 shorter events, 0.3 us)
Async XLA Ops:
  0.6 198.3 %copy-start = (bf16[192,2880]{1,0:T(8,128)(2,1)S(1)}, bf16[192,2880]{1,0:T(8,128)(2,1)}, u32[]{:S(2)}) copy-start(bf16[192,2880]{1,0:T(8,128)(2,1)} %param.8) | copy-start | bytes 3317764
  16.4 47.9 %all-to-all-start = ((bf16[32,1,4,1,4,2880]{5,4,2,3,1,0:T(4,128)(2,1)}), bf16[32,1,4,1,4,2880]{5,4,2,3,1,0:T(4,128)(2,1)}, u32[]{:S(2)}, u32[]{:S(2)}) async-start(bf16[32,1,4,1,4,2880]{5,4,2,3,1,0:T(4,128)(2,1)} %split.8), calls=%async_computation | async-start | bytes 6029312 | tf_op jit(solution)/shard_map/all_to_all | solution.py:40
  35.6 34.6 %copy-start.3 = (s32[192,4]{0,1:T(4,128)S(1)}, s32[192,4]{0,1:T(4,128)}, u32[]{:S(2)}) copy-start(s32[192,4]{0,1:T(4,128)} %param.9) | copy-start | bytes 9220
  35.6 36.0 %copy-start.1 = (bf16[192,2880]{1,0:T(8,128)(2,1)S(1)}, bf16[192,2880]{1,0:T(8,128)(2,1)}, u32[]{:S(2)}) copy-start(bf16[192,2880]{1,0:T(8,128)(2,1)} %param.7) | copy-start | bytes 3317764
  35.6 36.0 %copy-start.2 = (bf16[2880,128]{1,0:T(8,128)(2,1)S(1)}, bf16[2880,128]{1,0:T(8,128)(2,1)}, u32[]{:S(2)}) copy-start(bf16[2880,128]{1,0:T(8,128)(2,1)} %param.11) | copy-start | bytes 2211844
  35.7 36.0 %copy-start.4 = (f32[128]{0:T(128)S(1)}, f32[128]{0:T(128)}, u32[]{:S(2)}) copy-start(f32[128]{0:T(128)} %param.12) | copy-start | bytes 1540
  64.3 80.7 %all-to-all-start.1 = ((bf16[32,1,4,1,5,2880]{5,2,4,3,1,0:T(4,128)(2,1)}), bf16[32,1,4,1,5,2880]{5,2,4,3,1,0:T(4,128)(2,1)}, u32[]{:S(2)}, u32[]{:S(2)}) async-start(bf16[32,1,4,1,5,2880]{5,2,4,3,1,0:T(4,128)(2,1)} %copy.65), calls=%async_computation.1 | async-start | bytes 7536640 | tf_op jit(solution)/shard_map/all_to_all | solution.py:40
  210.7 34.0 %all-to-all-start.2 = ((f32[4,720,128]{2,1,0:T(8,128)}), f32[4,720,128]{2,1,0:T(8,128)S(1)}, u32[]{:S(2)}, u32[]{:S(2)}) async-start(f32[4,720,128]{2,1,0:T(8,128)} %bitcast.37), calls=%async_computation.2 | async-start | bytes 2949120 | tf_op jit(solution)/shard_map/all_to_all | solution.py:46
  247.5 16.3 %all-to-all-start.3 = ((f32[32,720,4]{1,2,0:T(4,128)}), f32[32,720,4]{1,2,0:T(4,128)S(1)}, u32[]{:S(2)}, u32[]{:S(2)}) async-start(f32[32,720,4]{1,2,0:T(4,128)} %bitcast.9), calls=%async_computation.3 | async-start | bytes 786432 | tf_op jit(solution)/shard_map/all_to_all | solution.py:46
where the time goes:
time: 267 us; the launch traced here: 266 us
  blocking collectives  92.9 us (35%)
  local copies, waits for them, and re-layouts  81.6 us (31%)
  waiting for transfers between devices  36.3 us (14%)
  starting transfers between devices  24.3 us (9%)
  other arithmetic  13.8 us (5%)
  matrix products  13.4 us (5%)
  between operations  3.27 us (1%)
    psum x8, blocking collectives, by_axis(): return functools.reduce(lax.psum, axes, shard)  92.9 us
    all_to_all x2, waiting for transfers between devices, several_exchanges(): lax.all_to_all(share, axis, split_axis=0, concat_axis=0, tiled=True)  28.6 us
    gather x2, local copies, waits for them, and re-layouts, on_device(): picked = jnp.take(flat_rows, row_index, axis=0)  20.2 us
    all_to_all x2, starting transfers between devices, several_exchanges(): lax.all_to_all(share, axis, split_axis=0, concat_axis=0, tiled=True)  14.9 us
    split x3, local copies, waits for them, and re-layouts, several_exchanges(): jnp.split(blocks, cut_rows(blocks.shape[widest], pieces), axis=widest)  14.7 us
    another operation x1, local copies, waits for them, and re-layouts, on_device(): flat_rows = returned.reshape(experts * capacity, width)  13.9 us
    unnamed x11, local copies, waits for them, and re-layouts  10.7 us
    concatenate x1, other arithmetic, several_exchanges(): return in_order(jnp.concatenate(gathered, axis=widest), concat_dim)  10.2 us
  transfers between devices with their start and end apart: 4, of which 2 were waited for; matrix products, arithmetic and copies ran while one was open for 9% of the time, Pallas kernels for 0%

commit v1 on v0

v1 whole, which is shorter than its diff:
```python
import math

import jax
import jax.numpy as jnp
from jax import lax
from jax.experimental import pallas as pl
from jax.experimental.pallas import tpu as pltpu
from jax.sharding import Mesh
from jax.sharding import PartitionSpec as P

AXES = ("ep_0", "ep_1", "ep_2", "dp")
EP = AXES[:3]
MESH = pl.DeviceIdType.MESH
F32, BF16, I32 = jnp.float32, jnp.bfloat16, jnp.int32

D, E, T, K, CAP = 2880, 128, 192, 4, 9
DPAD = 2944
SPLIT = 1536
WIDTH = (SPLIT, DPAD - SPLIT)
PER = 27
ROWS = 112
ES = 4 * CAP
KQ = ES * 8
PIECES = (((0, 768), (768, 768)), ((0, 768), (768, 640)))
N = 2
BLK = 896
TOTAL = 24576


def dot(a, b, dims=((1,), (0,)), **kw):
    return lax.dot_general(a, b, (dims, ((), ())), preferred_element_type=F32, **kw)


def iota(shape, dim):
    return lax.broadcasted_iota(I32, shape, dim)


def kernel(
    tok_h, og_h, idx_h, ex_h, w_h, b_h, bs_s,
    tg_o, wt_o, loss_o,
    tokraw, tokp, ogfull, og0, og1, idxv, ev3, ev, wv, bv,
    snd0, snd1, tr0, tr1, ex0, ex1, tokr,
    cntsnd, cntr, cc_v, meta, metar, rowsel, acc, gbuf, pds, pdr,
    psb, psr1, psr2, psb2, xcs, xcr, xps, xpr,
    lt, pt, mixv, lgs, lgr, rss, rsr,
    loc, og_s, og_r, ex2_s, ex2_r, fw_s, ex1_s, own_s, exr,
    c1_s, c1_r, c2_s, c2_r, me_s, me_r, p1_s, p1_r, p2_s, p2_r,
    xc_s, xc_r, xp_s, xp_r, tk_s, tk_r, pd_s, pd_r, lg_s, lg_r, rs_s, rs_r,
):
    y, z, c, x = (lax.axis_index(a) for a in AXES)
    og, snd, tr, ex = (og0, og1), (snd0, snd1), (tr0, tr1), (ex0, ex1)
    m4 = lambda v: lax.rem(v + 4, 4)
    po = (z, y)
    pe = (y, z)
    other = 1 - c

    def at(dy=0, dz=0, cc=None, dx=0):
        return (m4(y + dy), m4(z + dz), c if cc is None else cc, m4(x + dx))

    og_dev = (lambda s: at(dz=s), lambda s: at(dy=s))
    ex_dev = (lambda s, cc: at(dy=s, cc=cc), lambda s, cc: at(dz=s, cc=cc))

    def remote(src, dst, ss, rs, dev):
        return pltpu.make_async_remote_copy(src_ref=src, dst_ref=dst, send_sem=ss, recv_sem=rs, device_id=dev, device_id_type=MESH)

    sent = []

    def send(*a):
        r = remote(*a)
        r.start()
        sent.append(r)

    def got(ref, sem):
        remote(ref, ref, sem, sem, at(dx=1)).wait_recv()

    loads = [
        pltpu.make_async_copy(idx_h, idxv, loc.at[0]),
        pltpu.make_async_copy(og_h, ogfull, loc.at[1]),
        pltpu.make_async_copy(tok_h, tokraw, loc.at[2]),
        pltpu.make_async_copy(w_h, wv, loc.at[3]),
        pltpu.make_async_copy(b_h, bv, loc.at[4]),
    ] + [pltpu.make_async_copy(ex_h.at[:, q * 8 : q * 8 + 8, :], ev3.at[q], loc.at[5 + q]) for q in range(4)]
    for l in loads:
        l.start()
    peers = [at(dy=a, dz=b) for a in range(4) for b in range(4) if a or b]
    peers += [at(dy=a, cc=other) for a in (1, 2, 3)] + [at(dz=a, cc=other) for a in (1, 2, 3)]
    peers += [at(cc=other)] + [at(dx=a, cc=k) for a in (1, 2, 3) for k in (c, other)]
    barrier = pltpu.get_barrier_semaphore()
    for p in peers:
        pl.semaphore_signal(barrier, inc=1, device_id=p, device_id_type=MESH)

    loads[0].wait()
    idx = idxv[...]
    ie = iota((E, T), 0)
    named = jnp.zeros((E, T), F32)
    for k in range(K):
        named += jnp.where(idx[k : k + 1, :] == ie, 1.0, 0.0)
    nb = named.astype(BF16)
    upper = jnp.where(iota((T, T), 0) < iota((T, T), 1), 1.0, 0.0).astype(BF16)
    ones_tt = jnp.ones((T, T), BF16)
    r_e, c_e = iota((E, E), 0), iota((E, E), 1)
    same_ep = jnp.where((r_e // 4 == c_e // 4) & (c_e < r_e), 1.0, 0.0).astype(BF16)
    ahead = dot(same_ep, nb).astype(BF16)
    rowpos = dot(nb, upper) + dot(ahead, ones_tt)
    cntsnd[...] = dot(jnp.ones((8, T), BF16), nb, ((1,), (1,)))
    meta[...] = jnp.full((8, 256), -1e6, F32)
    for k in range(K):
        ik = idx[k : k + 1, :]
        off = jnp.sum(jnp.where(ik == ie, rowpos, 0.0), axis=0, keepdims=True)
        ey, ez, ec = ik // 32, (ik // 8) % 4, (ik // 4) % 2
        for h, (ea, eb) in enumerate(((ey, ez), (ez, ey))):
            code = (eb * 1024 + (ea * 2 + ec) * ROWS + po[h] * PER).astype(F32) + off
            meta[4 * h + k : 4 * h + k + 1, 0:T] = code

    loads[1].wait()
    own_og = [pl.ds(pl.multiple_of(po[h] * T, T), T) for h in range(2)]
    og0[own_og[0], :] = ogfull[:, 0:SPLIT]
    og1[own_og[1], WIDTH[1] - 128 : WIDTH[1]] = jnp.zeros((T, 128), BF16)
    og1[own_og[1], 0 : D - SPLIT] = ogfull[:, SPLIT:D]
    pl.semaphore_wait(barrier, len(peers))

    zc = z * 2 + c
    cntr[y, zc] = cntsnd[...]
    zpeers = [(b, k) for b in (1, 2, 3) for k in (0, 1)] + [(0, 1)]
    zdev = lambda b, k: at(dz=b, cc=lax.rem(c + k, 2))
    for n, (b, k) in enumerate(zpeers):
        send(cntsnd, cntr.at[y, zc], c1_s.at[n], c1_r.at[zc], zdev(b, k))
    for h in range(2):
        for s in (1, 2, 3):
            send(meta, metar.at[h, po[h]], me_s.at[h, s - 1], me_r.at[h, po[h]], og_dev[h](s))

    def og_rows(pos, second):
        return pl.ds(pl.multiple_of(pos * T + second * 96, 32), 96)

    def og_send(h, d, m):
        where = og_rows(po[h], d ^ m)
        send(og[h].at[where, :], og[h].at[where, :], og_s.at[h, d, m], og_r.at[h, d, m], og_dev[h](1 - 2 * d))

    for h in range(2):
        for d in range(2):
            og_send(h, d, 0)

    for b, k in zpeers:
        src = m4(z + b) * 2 + lax.rem(c + k, 2)
        got(cntr.at[y, src], c1_r.at[src])
    for s in (1, 2, 3):
        send(cntr.at[y], cntr.at[y], c2_s.at[s - 1], c2_r.at[y], at(dy=s))
    for h in range(2):
        for d in range(2):
            og_send(h, d, 1)

    loads[2].wait()
    tokp[:, DPAD - 128 : DPAD] = jnp.zeros((T, 128), BF16)
    tokp[:, 0:D] = tokraw[...]

    def block(pos):
        return pl.ds(pl.multiple_of((pos * 720) // 128 * 128, 128), BLK)

    xc = x * 2 + c
    xpeers = [(a, k) for a in (1, 2, 3) for k in (0, 1)] + [(0, 1)]
    xdev = lambda a, k: at(dx=a, cc=lax.rem(c + k, 2))
    tokr[xc] = tokp[:, block(x)]
    for n, (a, k) in enumerate(xpeers):
        send(tokp.at[:, block(m4(x + a))], tokr.at[xc], tk_s.at[n], tk_r.at[xc], xdev(a, k))

    loads[3].wait()
    loads[4].wait()
    logits = jnp.transpose(dot(tokp[:, 0:D], wv[...]) + bv[...])
    lt[...] = logits
    ex_l = jnp.exp(logits - jnp.max(logits, axis=0, keepdims=True))
    prob = ex_l / jnp.sum(ex_l, axis=0, keepdims=True)
    pt[...] = prob
    picked = [jnp.sum(jnp.where(idx[k : k + 1, :] == ie, logits, 0.0), axis=0, keepdims=True) for k in range(K)]
    top = jnp.maximum(jnp.maximum(picked[0], picked[1]), jnp.maximum(picked[2], picked[3]))
    picked = [jnp.exp(p - top) for p in picked]
    total = picked[0] + picked[1] + picked[2] + picked[3]
    for k in range(K):
        mixv[k : k + 1, :] = picked[k] / total
    diag = r_e == c_e
    pcol = jnp.sum(prob, axis=1, keepdims=True)
    prow = jnp.sum(jnp.where(diag, pcol, 0.0), axis=0, keepdims=True)
    psb[...] = jnp.broadcast_to(prow, (8, E))
    for n, (b, k) in enumerate(zpeers):
        send(psb, psr1.at[zc], p1_s.at[n], p1_r.at[zc], zdev(b, k))
    psr1[zc] = psb[...]

    for q in range(4):
        loads[5 + q].wait()
    ev[:, DPAD - 128 : DPAD] = jnp.zeros((4 * KQ, 128), BF16)

    def flatten(n, _):
        q, p = n // (ES // 2), lax.rem(n, ES // 2)
        pair = jnp.concatenate([ev3[q, 2 * p], ev3[q, 2 * p + 1]], axis=0)
        ev[pl.ds(pl.multiple_of(n * 16, 16), 16), 0:D] = pair
        return 0

    lax.fori_loop(0, 4 * ES // 2, flatten, 0)

    def og_from(d, h):
        return m4(po[h] - (1 - 2 * d))

    for h in range(2):
        for d in range(2):
            where = og_rows(og_from(d, h), d)
            got(og[h].at[where, :], og_r.at[h, d, 0])
            send(og[h].at[where, :], og[h].at[where, :], og_s.at[h, d, 2], og_r.at[h, d, 2], og_dev[h](1 - 2 * d))

    for s in (1, 2, 3):
        got(cntr.at[m4(y + s)], c2_r.at[m4(y + s)])
    counts = cntr[...]
    plane = jnp.sum(counts.reshape(32, 8, E), axis=0)
    xcs[...] = plane
    xcr[x] = plane
    for a in (1, 2, 3):
        send(xcs, xcr.at[x], xc_s.at[a - 1], xc_r.at[x], at(dx=a))
    first = (y * 8 + z * 2 + c) * 4
    cb = counts.reshape(256, E).astype(BF16)
    for k in range(K):
        mine = jnp.where((r_e >= first) & (r_e <= first + k), 1.0, 0.0).astype(BF16)
        cc_v[k] = dot(cb, mine).astype(BF16)

    def gather(h, delta):
        q = m4(pe[h] + delta)
        row = iota((2 * ROWS, E), 0)
        core = jnp.where(row >= ROWS, 1, 0)
        rr = row - core * ROWS
        i = jnp.where(rr >= PER, 1, 0) + jnp.where(rr >= 2 * PER, 1, 0) + jnp.where(rr >= 3 * PER, 1, 0)
        r = rr - i * PER
        dev = (q * 8 + i * 2 + core) if h == 0 else (i * 8 + q * 2 + core)
        pick = (jnp.broadcast_to(dev[:, 0:1] * 8, (2 * ROWS, 256)) == iota((2 * ROWS, 256), 1))
        pick = jnp.where(pick, 1.0, 0.0).astype(BF16)
        t = [dot(pick, cc_v[k]).astype(I32) for k in range(K)]
        e_in = jnp.where(r >= t[0], 1, 0) + jnp.where(r >= t[1], 1, 0) + jnp.where(r >= t[2], 1, 0)
        base = jnp.where(r >= t[2], t[2], jnp.where(r >= t[1], t[1], jnp.where(r >= t[0], t[0], 0)))
        es = e_in * CAP + r - base
        target = (es * 8 + i * 2 + core) if h == 0 else (i * KQ + es * 8 + q * 2 + core)
        target = jnp.where((r < t[3]) & (rr < 4 * PER), target, -1)
        depth = KQ if h == 0 else 4 * KQ
        sel = jnp.broadcast_to(target[:, 0:1], (2 * ROWS, depth)) == iota((2 * ROWS, depth), 1)
        sel = jnp.where(sel, 1.0, 0.0).astype(BF16)
        rows = pl.ds(pl.multiple_of(q * KQ, KQ), KQ) if h == 0 else pl.ds(0, 4 * KQ)
        for lo, w in PIECES[h]:
            snd[h][delta, :, lo : lo + w] = dot(sel, ev[rows, h * SPLIT + lo : h * SPLIT + lo + w]).astype(BF16)

    def core_rows(cc):
        return pl.ds(pl.multiple_of(cc * ROWS, 16), ROWS)

    def cols(h, n):
        return pl.ds(PIECES[h][n][0], PIECES[h][n][1])

    for h in range(2):
        gather(h, 2)
        for d in range(2):
            for n in range(N):
                send(
                    snd[h].at[2, core_rows(d), cols(h, n)], tr[h].at[d, :, cols(h, n)],
                    ex2_s.at[h, d, n], ex2_r.at[h, d, n], ex_dev[h](1 - 2 * d, c),
                )

    def gather_rest(o, _):
        delta = jnp.where(o == 0, 1, jnp.where(o == 1, 3, 0))
        gather(0, delta)
        gather(1, delta)
        return 0

    lax.fori_loop(0, 3, gather_rest, 0)

    def ex1_send(slot):
        cc = c if slot == 0 else other
        for n in range(N):
            for h in range(2):
                for d in range(2):
                    send(
                        snd[h].at[1 + 2 * d, core_rows(cc), cols(h, n)], ex[h].at[pe[h] * 2 + c, :, cols(h, n)],
                        ex1_s.at[h, d, slot, n], exr.at[h, pe[h] * 2 + c, n], ex_dev[h](1 - 2 * d, cc),
                    )

    ex1_send(0)
    for h in range(2):
        for n in range(N):
            send(
                snd[h].at[0, core_rows(other), cols(h, n)], ex[h].at[pe[h] * 2 + c, :, cols(h, n)],
                own_s.at[h, n], exr.at[h, pe[h] * 2 + c, n], at(cc=other),
            )
        ex[h][pe[h] * 2 + c] = snd[h][0, core_rows(c), :]

    for h in range(2):
        for s in (1, 2, 3):
            got(metar.at[h, m4(po[h] + s)], me_r.at[h, m4(po[h] + s)])
        metar[h, po[h]] = meta[...]
        for i in range(4):
            rowsel[h, :, i * T : (i + 1) * T] = metar[h, i, 4 * h : 4 * h + 4, 0:T] - (pe[1 - h] * 1024).astype(F32)
        for d in range(2):
            got(og[h].at[og_rows(og_from(d, h), 1 - d), :], og_r.at[h, d, 1])
            got(og[h].at[og_rows(m4(po[h] + 2), d), :], og_r.at[h, d, 2])
    acc[...] = jnp.zeros_like(acc)

    def absorb(h, src, here):
        for n in range(N):
            if not here:
                got(ex[h].at[src, :, cols(h, n)], exr.at[h, src, n])
            lo, w = PIECES[h][n]
            part = dot(ex[h][src, :, lo : lo + w], og[h][:, lo : lo + w], ((1,), (1,)))
            if n == 0:
                gbuf[...] = part
            else:
                gbuf[...] += part
        rid = (iota((ROWS, 128), 0) + src * ROWS).astype(F32)
        for lb in range(6):
            lanes = slice(lb * 128, lb * 128 + 128)
            g = gbuf[:, lanes]
            for k in range(K):
                hit = jnp.where(rid == rowsel[h, k : k + 1, lanes], g, 0.0)
                acc[h, k, :, lanes] += jnp.sum(hit.reshape(ROWS // 8, 8, 128), axis=0)

    for h in range(2):
        absorb(h, pe[h] * 2 + c, True)

    for n in range(N):
        for h in range(2):
            for d in range(2):
                got(tr[h].at[d, :, cols(h, n)], ex2_r.at[h, d, n])
                src = m4(pe[h] - (1 - 2 * d)) * 2 + c
                send(
                    tr[h].at[d, :, cols(h, n)], ex[h].at[src, :, cols(h, n)],
                    fw_s.at[h, d, n], exr.at[h, src, n], ex_dev[h](1 - 2 * d, d),
                )
    ex1_send(1)

    for b, k in zpeers:
        src = m4(z + b) * 2 + lax.rem(c + k, 2)
        got(psr1.at[src], p1_r.at[src])
    psb2[...] = jnp.sum(psr1[...], axis=0)
    psr2[y] = psb2[...]
    for s in (1, 2, 3):
        send(psb2, psr2.at[y], p2_s.at[s - 1], p2_r.at[y], at(dy=s))

    for a in (1, 2, 3):
        got(xcr.at[m4(x + a)], xc_r.at[m4(x + a)])
    cnt_row = jnp.sum(xcr[...], axis=0)[0:1, :]
    cnt_col = jnp.sum(jnp.where(diag, cnt_row, 0.0), axis=1, keepdims=True)
    push = bs_s[0] * E * (cnt_col / (TOTAL * K))
    prob = pt[...]
    lt[...] = prob * (push - jnp.sum(prob * push, axis=0, keepdims=True))

    def arrivals(o, _):
        g, o2 = (o + 1) // 2, lax.rem(o + 1, 2)
        step = jnp.where(g == 0, 0, jnp.where(g == 2, 2, 1 + 2 * o2))
        core = jnp.where(g == 1, c, jnp.where(g == 2, o2, other))
        for h in range(2):
            absorb(h, m4(pe[h] + step) * 2 + core, False)
        return 0

    lax.fori_loop(0, 7, arrivals, 0)

    for h in range(2):
        for i in range(4):
            pds[h, i] = jnp.zeros((8, 256), F32)
            for k in range(K):
                pds[h, i, k : k + 1, 0:T] = jnp.sum(acc[h, k, :, i * T : (i + 1) * T], axis=0, keepdims=True)
        for s in (1, 2, 3):
            send(pds.at[h, m4(po[h] + s)], pdr.at[h, po[h]], pd_s.at[h, s - 1], pd_r.at[h, po[h]], og_dev[h](s))
        pdr[h, po[h]] = pds[h, po[h]]
    for s in (1, 2, 3):
        got(psr2.at[m4(y + s)], p2_r.at[m4(y + s)])
    xps[...] = jnp.sum(psr2[...], axis=0)
    xpr[x] = xps[...]
    for a in (1, 2, 3):
        send(xps, xpr.at[x], xp_s.at[a - 1], xp_r.at[x], at(dx=a))
    pd = jnp.zeros((8, 256), F32)
    for h in range(2):
        for s in (1, 2, 3):
            got(pdr.at[h, m4(po[h] + s)], pd_r.at[h, m4(po[h] + s)])
        pd += (pdr[h, 0] + pdr[h, 1]) + (pdr[h, 2] + pdr[h, 3])

    dots = [pd[k : k + 1, 0:T] for k in range(K)]
    mix = [mixv[k : k + 1, :] for k in range(K)]
    mean = mix[0] * dots[0] + mix[1] * dots[1] + mix[2] * dots[2] + mix[3] * dots[3]
    lg = lt[...]
    named = jnp.zeros((E, T), F32)
    for k in range(K):
        named += jnp.where(idxv[k : k + 1, :] == ie, mix[k] * (dots[k] - mean), 0.0)
    lg = lg + named
    lgb = lg.astype(BF16)
    for par in range(2):
        rs_, cs_ = iota((64, E), 0), iota((64, E), 1)
        perm = jnp.where(cs_ == (rs_ // 4) * 8 + par * 4 + rs_ % 4, 1.0, 0.0).astype(BF16)
        lgs[par, :, 0:T] = dot(perm, lgb).astype(BF16)
        lgs[par, :, T:256] = jnp.zeros((64, 256 - T), BF16)
    for n, (a, k) in enumerate(xpeers):
        cc = lax.rem(c + k, 2)
        send(lgs.at[cc], lgr.at[xc], lg_s.at[n], lg_r.at[xc], xdev(a, k))
    lgr[xc] = lgs[c]

    lgt = jnp.transpose(lg).astype(BF16)
    tg_o[...] = dot(lgt, wv[...], ((1,), (1,))).astype(BF16)

    for a, k in xpeers:
        src = m4(x + a) * 2 + lax.rem(c + k, 2)
        got(tokr.at[src], tk_r.at[src])
    wsum = dot(lgr[xc][:, 0:T], tokr[xc])
    for a, k in xpeers:
        src = m4(x + a) * 2 + lax.rem(c + k, 2)
        got(lgr.at[src], lg_r.at[src])
        wsum += dot(lgr[src][:, 0:T], tokr[src])
    for n in range(16):
        rss[n] = wsum[4 * n : 4 * n + 4, :]
    chip = y * 4 + z
    n = 0
    for a in range(4):
        for b in range(4):
            if a or b:
                dest = m4(y + a) * 4 + m4(z + b)
                send(rss.at[dest], rsr.at[chip], rs_s.at[n], rs_r.at[chip], at(dy=a, dz=b))
                n += 1
    rsr[chip] = rss[chip]

    for a in (1, 2, 3):
        got(xpr.at[m4(x + a)], xp_r.at[m4(x + a)])
    ps_row = jnp.sum(xpr[...], axis=0)[0:1, :]
    loss_o[0] = E * jnp.sum((cnt_row / (TOTAL * K)) * (ps_row / TOTAL))

    for a in range(4):
        for b in range(4):
            if a or b:
                src = m4(y + a) * 4 + m4(z + b)
                got(rsr.at[src], rs_r.at[src])
    out = jnp.sum(rsr[...], axis=0) * (1.0 / math.sqrt(TOTAL))
    out = jnp.concatenate([out, out], axis=0)
    shift = x * 720 - (x * 720) // 128 * 128
    out = pltpu.roll(out, lax.rem(BLK - shift, BLK), 1)
    wt_o[...] = out[0:4, 0:720]
    for s in sent:
        s.wait_send()


def on_device(tokens, out_grad, indices, expert_rows, router_weight, router_bias, balance_scale):
    rows = jnp.transpose(expert_rows[0], (0, 2, 1, 3)).reshape(ES, 32, D)
    dma = pltpu.SemaphoreType.DMA
    vm = pltpu.VMEM
    scratch = [
        vm((T, D), BF16), vm((T, DPAD), BF16), vm((T, D), BF16), vm((4 * T, WIDTH[0]), BF16), vm((4 * T, WIDTH[1]), BF16),
        vm((K, T), I32), vm((4, ES, 8, D), BF16), vm((4 * KQ, DPAD), BF16), vm((D, E), BF16), vm((1, E), F32),
        vm((4, 2 * ROWS, WIDTH[0]), BF16), vm((4, 2 * ROWS, WIDTH[1]), BF16),
        vm((2, ROWS, WIDTH[0]), BF16), vm((2, ROWS, WIDTH[1]), BF16),
        vm((8, ROWS, WIDTH[0]), BF16), vm((8, ROWS, WIDTH[1]), BF16), vm((8, T, BLK), BF16),
        vm((8, E), F32), vm((4, 8, 8, E), F32), vm((K, 256, E), BF16), vm((8, 256), F32), vm((2, 4, 8, 256), F32),
        vm((2, K, 4 * T), F32), vm((2, K, 8, 4 * T), F32), vm((ROWS, 4 * T), F32), vm((2, 4, 8, 256), F32), vm((2, 4, 8, 256), F32),
        vm((8, E), F32), vm((8, 8, E), F32), vm((4, 8, E), F32), vm((8, E), F32),
        vm((8, E), F32), vm((4, 8, E), F32), vm((8, E), F32), vm((4, 8, E), F32),
        vm((E, T), F32), vm((E, T), F32), vm((K, T), F32), vm((2, 64, 256), BF16), vm((8, 64, 256), BF16),
        vm((16, 4, BLK), F32), vm((16, 4, BLK), F32),
        dma((9,)), dma((2, 2, 3)), dma((2, 2, 3)), dma((2, 2, N)), dma((2, 2, N)), dma((2, 2, N)), dma((2, 2, 2, N)), dma((2, N)), dma((2, 8, N)),
        dma((7,)), dma((8,)), dma((3,)), dma((4,)), dma((2, 3)), dma((2, 4)), dma((7,)), dma((8,)), dma((3,)), dma((4,)),
        dma((3,)), dma((4,)), dma((3,)), dma((4,)), dma((7,)), dma((8,)), dma((2, 3)), dma((2, 4)), dma((7,)), dma((8,)), dma((15,)), dma((16,)),
    ]
    hbm = pl.BlockSpec(memory_space=pl.ANY)
    token_grad, weight_grad, loss = pl.pallas_call(
        kernel,
        out_shape=(
            jax.ShapeDtypeStruct((T, D), BF16),
            jax.ShapeDtypeStruct((4, 720), F32),
            jax.ShapeDtypeStruct((1,), F32),
        ),
        in_specs=[hbm] * 6 + [pl.BlockSpec(memory_space=pltpu.SMEM)],
        out_specs=(
            pl.BlockSpec(memory_space=pltpu.VMEM),
            pl.BlockSpec(memory_space=pltpu.VMEM),
            pl.BlockSpec(memory_space=pltpu.SMEM),
        ),
        scratch_shapes=scratch,
        compiler_params=pltpu.CompilerParams(collective_id=0, has_side_effects=True, vmem_limit_bytes=64000 * 1024),
        name="router",
    )(tokens, out_grad, indices.T, rows, router_weight, router_bias.reshape(1, E), balance_scale)
    return token_grad, weight_grad.T, loss


def solution(mesh):
    torus = Mesh(mesh.devices.reshape(4, 4, 2, mesh.shape["dp"]), AXES)
    return jax.shard_map(
        on_device,
        mesh=torus,
        in_specs=(P(AXES, None), P(AXES, None), P(AXES, None), P("dp", EP, None, None, None), P(), P(), P()),
        out_specs=(P(AXES, None), P("dp", EP), P()),
        check_vma=False,
    )
```

time: 267 us -> 87.4 us (0.33)
  blocking collectives: 92.9 us -> 0 us
  Pallas kernels: 0 us -> 80.9 us
  local copies, waits for them, and re-layouts: 81.6 us -> 2.94 us
  waiting for transfers between devices: 36.3 us -> 0 us
  starting transfers between devices: 24.3 us -> 0 us
  other arithmetic: 13.8 us -> 0 us
  matrix products: 13.4 us -> 0 us
    psum x8 -> x0, blocking collectives: 92.9 us -> none  [by_axis(): return functools.reduce(lax.psum, axes, shard)]
    pallas_call x0 -> x1, Pallas kernels: none -> 80.9 us  [on_device(): pl.pallas_call(kernel, out_shape=(jax.ShapeDtypeStruct((T, D), BF16), jax...]
    all_to_all x4 -> x0, waiting for transfers between devices: 36.3 us -> none  [the longest x2 28.6 us: several_exchanges(): lax.all_to_all(share, axis, split_axis=0, concat_axis=0, tiled=True)]
    gather x7 -> x0, local copies, waits for them, and re-layouts: 25.6 us -> none  [the longest x2 20.2 us: on_device(): picked = jnp.take(flat_rows, row_index, axis=0)]
    all_to_all x4 -> x0, starting transfers between devices: 24.3 us -> none  [the longest x2 14.9 us: several_exchanges(): lax.all_to_all(share, axis, split_axis=0, concat_axis=0, tiled=True)]
    split x3 -> x0, local copies, waits for them, and re-layouts: 14.7 us -> none  [several_exchanges(): jnp.split(blocks, cut_rows(blocks.shape[widest], pieces), axis=widest)]
    another operation x1 -> x0, local copies, waits for them, and re-layouts: 13.9 us -> none  [on_device(): flat_rows = returned.reshape(experts * capacity, width)]
    dot_general x5 -> x0, matrix products: 13.4 us -> none  [the longest x1 9.39 us: on_device(): jnp.einsum('td,tkd->tk', out_grad, picked, preferred_element_type=jnp.flo...]
  transfers between devices with their start and end apart: 4 -> 0, of which waited for: 2 -> 0; matrix products, arithmetic and copies ran while one was open for 9% -> 0% of each run, Pallas kernels for 0% -> 0%
where the time goes in v1:
time: 87.4 us; the launch traced here: 86.9 us
  Pallas kernels  80.9 us (93%)
  between operations  3.04 us (3%)
  local copies, waits for them, and re-layouts  2.94 us (3%)
    pallas_call x1, Pallas kernels, on_device(): pl.pallas_call(kernel, out_shape=(jax.ShapeDtypeStruct((T, D), BF16), jax...  80.9 us
    unnamed x4, local copies, waits for them, and re-layouts  2.94 us

profile of v1, /device:TPU:1, one launch (start us, length us, event | category | flops | bytes accessed | tf_op | source)
XLA Modules:
  0.0 86.9 jit_solution(18396027719336903962)
XLA Ops:
  1.3 80.9 %router.1 = (bf16[192,2880]{1,0:T(8,128)(2,1)}, f32[4,720]{1,0:T(4,128)}, f32[1]{0:T(128)}) custom-call(bf16[192,2880]{1,0:T(8,128)(2,1)} %tok_h.1, bf16[192,2880]{1,0:T(8,128)(2,1)} %og_h.1, s32[4,192]{1,0:T(4,128)} %bitcast.10, bf16[36,32,2880]{2,1,0:T(8,128)(2,1)} %bitcast.8, bf16[2880,128]{1,0:T(8,128)(2,1)} %w_h.1, f32[1,128]{1,0:T(1,128)} %bitcast.11, ...), custom_call_target="tpu_custom_call" | custom-call | tf_op jit(solution)/shard_map/router/pallas_call | solution.py:458
  82.2 0.0 copy-start
  82.2 2.3 %copy.14 = bf16[192,2880]{1,0:T(8,128)(2,1)} copy(bf16[192,2880]{1,0:T(8,128)(2,1)} %get-tuple-element.12) | data formatting | bytes 2211840
  84.6 0.0 copy-done
  84.6 0.6 copy.15
Async XLA Ops:
  82.2 2.3 %copy-start = (f32[4,720]{1,0:T(4,128)S(1)}, f32[4,720]{1,0:T(4,128)}, u32[]{:S(2)}) copy-start(f32[4,720]{1,0:T(4,128)} %get-tuple-element.7) | copy-start | bytes 34564

commit v2 on v1

--- a/solution.py
+++ b/solution.py
@@ -21,9 +21,10 @@
 ROWS = 112
 ES = 4 * CAP
 KQ = ES * 8
-PIECES = (((0, 768), (768, 768)), ((0, 768), (768, 640)))
-N = 2
+PIECES = (((0, 640), (640, 512), (1152, 384)), ((0, 640), (640, 512), (1152, 256)))
+N = 3
 BLK = 896
+OUT = 768
 TOTAL = 24576
 
 
@@ -36,16 +37,16 @@
 
 
 def kernel(
-    tok_h, og_h, idx_h, ex_h, w_h, b_h, bs_s,
-    tg_o, wt_o, loss_o,
+    tok_h, og_h, idx_h, ex_h, w_h, b_h, bs_h,
+    lg_o, wt_o, loss_o,
     tokraw, tokp, ogfull, og0, og1, idxv, ev3, ev, wv, bv,
     snd0, snd1, tr0, tr1, ex0, ex1, tokr,
     cntsnd, cntr, cc_v, meta, metar, rowsel, acc, gbuf, pds, pdr,
     psb, psr1, psr2, psb2, xcs, xcr, xps, xpr,
-    lt, pt, mixv, lgs, lgr, rss, rsr,
+    lt, pt, mixv, spb, spr, selb, selr, rss, rsr, bs_s,
     loc, og_s, og_r, ex2_s, ex2_r, fw_s, ex1_s, own_s, exr,
     c1_s, c1_r, c2_s, c2_r, me_s, me_r, p1_s, p1_r, p2_s, p2_r,
-    xc_s, xc_r, xp_s, xp_r, tk_s, tk_r, pd_s, pd_r, lg_s, lg_r, rs_s, rs_r,
+    xc_s, xc_r, xp_s, xp_r, tk_s, tk_r, pd_s, pd_r, sp_s, sp_r, lg_s, lg_r, rs_s, rs_r,
 ):
     y, z, c, x = (lax.axis_index(a) for a in AXES)
     og, snd, tr, ex = (og0, og1), (snd0, snd1), (tr0, tr1), (ex0, ex1)
@@ -80,6 +81,7 @@
         pltpu.make_async_copy(w_h, wv, loc.at[3]),
         pltpu.make_async_copy(b_h, bv, loc.at[4]),
     ] + [pltpu.make_async_copy(ex_h.at[:, q * 8 : q * 8 + 8, :], ev3.at[q], loc.at[5 + q]) for q in range(4)]
+    loads.append(pltpu.make_async_copy(bs_h, bs_s, loc.at[9]))
     for l in loads:
         l.start()
     peers = [at(dy=a, dz=b) for a in range(4) for b in range(4) if a or b]
@@ -109,7 +111,10 @@
         off = jnp.sum(jnp.where(ik == ie, rowpos, 0.0), axis=0, keepdims=True)
         ey, ez, ec = ik // 32, (ik // 8) % 4, (ik // 4) % 2
         for h, (ea, eb) in enumerate(((ey, ez), (ez, ey))):
-            code = (eb * 1024 + (ea * 2 + ec) * ROWS + po[h] * PER).astype(F32) + off
+            step, same = (ea - pe[h] + 4) % 4, ec == c
+            near = jnp.where(step == 1, jnp.where(same, 2, 6), jnp.where(same, 3, 7))
+            slot = jnp.where(step == 0, jnp.where(same, 0, 1), jnp.where(step == 2, 4 + ec, near))
+            code = (eb * 1024 + slot * ROWS + po[h] * PER).astype(F32) + off
             meta[4 * h + k : 4 * h + k + 1, 0:T] = code
 
     loads[1].wait()
@@ -271,18 +276,18 @@
             for h in range(2):
                 for d in range(2):
                     send(
-                        snd[h].at[1 + 2 * d, core_rows(cc), cols(h, n)], ex[h].at[pe[h] * 2 + c, :, cols(h, n)],
-                        ex1_s.at[h, d, slot, n], exr.at[h, pe[h] * 2 + c, n], ex_dev[h](1 - 2 * d, cc),
+                        snd[h].at[1 + 2 * d, core_rows(cc), cols(h, n)], ex[h].at[3 - d + 4 * slot, :, cols(h, n)],
+                        ex1_s.at[h, d, slot, n], exr.at[h, 3 - d + 4 * slot, n], ex_dev[h](1 - 2 * d, cc),
                     )
 
     ex1_send(0)
     for h in range(2):
         for n in range(N):
             send(
-                snd[h].at[0, core_rows(other), cols(h, n)], ex[h].at[pe[h] * 2 + c, :, cols(h, n)],
-                own_s.at[h, n], exr.at[h, pe[h] * 2 + c, n], at(cc=other),
+                snd[h].at[0, core_rows(other), cols(h, n)], ex[h].at[1, :, cols(h, n)],
+                own_s.at[h, n], exr.at[h, 1, n], at(cc=other),
             )
-        ex[h][pe[h] * 2 + c] = snd[h][0, core_rows(c), :]
+        ex[h][0] = snd[h][0, core_rows(c), :]
 
     for h in range(2):
         for s in (1, 2, 3):
@@ -295,35 +300,36 @@
             got(og[h].at[og_rows(m4(po[h] + 2), d), :], og_r.at[h, d, 2])
     acc[...] = jnp.zeros_like(acc)
 
-    def absorb(h, src, here):
+    def absorb(pair, mine):
         for n in range(N):
-            if not here:
-                got(ex[h].at[src, :, cols(h, n)], exr.at[h, src, n])
-            lo, w = PIECES[h][n]
-            part = dot(ex[h][src, :, lo : lo + w], og[h][:, lo : lo + w], ((1,), (1,)))
-            if n == 0:
-                gbuf[...] = part
-            else:
-                gbuf[...] += part
-        rid = (iota((ROWS, 128), 0) + src * ROWS).astype(F32)
-        for lb in range(6):
-            lanes = slice(lb * 128, lb * 128 + 128)
-            g = gbuf[:, lanes]
-            for k in range(K):
-                hit = jnp.where(rid == rowsel[h, k : k + 1, lanes], g, 0.0)
-                acc[h, k, :, lanes] += jnp.sum(hit.reshape(ROWS // 8, 8, 128), axis=0)
-
-    for h in range(2):
-        absorb(h, pe[h] * 2 + c, True)
+            for h in range(2):
+                for slot in (1,) if mine else (0, 1):
+                    got(ex[h].at[2 * pair + slot, :, cols(h, n)], exr.at[h, 2 * pair + slot, n])
+                lo, w = PIECES[h][n]
+                block = ex[h][pl.ds(2 * pair, 2), :, lo : lo + w].reshape(2 * ROWS, w)
+                part = dot(block, og[h][:, lo : lo + w], ((1,), (1,)))
+                if n == 0:
+                    gbuf[h] = part
+                else:
+                    gbuf[h] += part
+        rid = (iota((2 * ROWS, 128), 0) + pair * 2 * ROWS).astype(F32)
+        for h in range(2):
+            for lb in range(6):
+                lanes = slice(lb * 128, lb * 128 + 128)
+                g = gbuf[h, :, lanes]
+                for k in range(K):
+                    hit = jnp.where(rid == rowsel[h, k : k + 1, lanes], g, 0.0)
+                    acc[h, k, :, lanes] += jnp.sum(hit.reshape(2 * ROWS // 8, 8, 128), axis=0)
+
+    absorb(0, True)
 
     for n in range(N):
         for h in range(2):
             for d in range(2):
                 got(tr[h].at[d, :, cols(h, n)], ex2_r.at[h, d, n])
-                src = m4(pe[h] - (1 - 2 * d)) * 2 + c
                 send(
-                    tr[h].at[d, :, cols(h, n)], ex[h].at[src, :, cols(h, n)],
-                    fw_s.at[h, d, n], exr.at[h, src, n], ex_dev[h](1 - 2 * d, d),
+                    tr[h].at[d, :, cols(h, n)], ex[h].at[4 + c, :, cols(h, n)],
+                    fw_s.at[h, d, n], exr.at[h, 4 + c, n], ex_dev[h](1 - 2 * d, d),
                 )
     ex1_send(1)
 
@@ -339,23 +345,31 @@
         got(xcr.at[m4(x + a)], xc_r.at[m4(x + a)])
     cnt_row = jnp.sum(xcr[...], axis=0)[0:1, :]
     cnt_col = jnp.sum(jnp.where(diag, cnt_row, 0.0), axis=1, keepdims=True)
+    loads[9].wait()
     push = bs_s[0] * E * (cnt_col / (TOTAL * K))
     prob = pt[...]
-    lt[...] = prob * (push - jnp.sum(prob * push, axis=0, keepdims=True))
-
-    def arrivals(o, _):
-        g, o2 = (o + 1) // 2, lax.rem(o + 1, 2)
-        step = jnp.where(g == 0, 0, jnp.where(g == 2, 2, 1 + 2 * o2))
-        core = jnp.where(g == 1, c, jnp.where(g == 2, o2, other))
-        for h in range(2):
-            absorb(h, m4(pe[h] + step) * 2 + core, False)
+    spread = prob * (push - jnp.sum(prob * push, axis=0, keepdims=True))
+    lt[...] = spread
+    spb[...] = jnp.zeros_like(spb)
+    for par in range(2):
+        for n in range(16):
+            spb[par, 4 * n : 4 * n + 4, 0:T] = spread[8 * n + 4 * par : 8 * n + 4 * par + 4, :]
+        for k in range(K):
+            ik = idxv[k : k + 1, :]
+            spb[par, 64 + k : 65 + k, 0:T] = jnp.where((ik // 4) % 2 == par, ik // 8 * 4 + ik % 4, -1).astype(F32)
+    for n, (a, k) in enumerate(xpeers):
+        send(spb.at[lax.rem(c + k, 2)], spr.at[xc], sp_s.at[n], sp_r.at[xc], xdev(a, k))
+    spr[xc] = spb[c]
+
+    def arrivals(pair, _):
+        absorb(pair, False)
         return 0
 
-    lax.fori_loop(0, 7, arrivals, 0)
+    lax.fori_loop(1, 4, arrivals, 0)
 
     for h in range(2):
         for i in range(4):
-            pds[h, i] = jnp.zeros((8, 256), F32)
+            pds[h, i] = jnp.zeros((K, 256), F32)
             for k in range(K):
                 pds[h, i, k : k + 1, 0:T] = jnp.sum(acc[h, k, :, i * T : (i + 1) * T], axis=0, keepdims=True)
         for s in (1, 2, 3):
@@ -367,7 +381,7 @@
     xpr[x] = xps[...]
     for a in (1, 2, 3):
         send(xps, xpr.at[x], xp_s.at[a - 1], xp_r.at[x], at(dx=a))
-    pd = jnp.zeros((8, 256), F32)
+    pd = jnp.zeros((K, 256), F32)
     for h in range(2):
         for s in (1, 2, 3):
             got(pdr.at[h, m4(po[h] + s)], pd_r.at[h, m4(po[h] + s)])
@@ -376,43 +390,44 @@
     dots = [pd[k : k + 1, 0:T] for k in range(K)]
     mix = [mixv[k : k + 1, :] for k in range(K)]
     mean = mix[0] * dots[0] + mix[1] * dots[1] + mix[2] * dots[2] + mix[3] * dots[3]
-    lg = lt[...]
-    named = jnp.zeros((E, T), F32)
-    for k in range(K):
-        named += jnp.where(idxv[k : k + 1, :] == ie, mix[k] * (dots[k] - mean), 0.0)
-    lg = lg + named
-    lgb = lg.astype(BF16)
-    for par in range(2):
-        rs_, cs_ = iota((64, E), 0), iota((64, E), 1)
-        perm = jnp.where(cs_ == (rs_ // 4) * 8 + par * 4 + rs_ % 4, 1.0, 0.0).astype(BF16)
-        lgs[par, :, 0:T] = dot(perm, lgb).astype(BF16)
-        lgs[par, :, T:256] = jnp.zeros((64, 256 - T), BF16)
+    for k in range(K):
+        selb[k : k + 1, 0:T] = mix[k] * (dots[k] - mean)
+    selb[:, T:256] = jnp.zeros((K, 256 - T), F32)
     for n, (a, k) in enumerate(xpeers):
-        cc = lax.rem(c + k, 2)
-        send(lgs.at[cc], lgr.at[xc], lg_s.at[n], lg_r.at[xc], xdev(a, k))
-    lgr[xc] = lgs[c]
-
-    lgt = jnp.transpose(lg).astype(BF16)
-    tg_o[...] = dot(lgt, wv[...], ((1,), (1,))).astype(BF16)
-
+        send(selb, selr.at[xc], lg_s.at[n], lg_r.at[xc], xdev(a, k))
+
+    lg = jnp.zeros((E, T), F32)
+    for k in range(K):
+        lg += jnp.where(idxv[k : k + 1, :] == ie, selb[k : k + 1, 0:T], 0.0)
+    lg_o[...] = jnp.transpose(lt[...] + lg).astype(BF16)
     for a, k in xpeers:
         src = m4(x + a) * 2 + lax.rem(c + k, 2)
         got(tokr.at[src], tk_r.at[src])
-    wsum = dot(lgr[xc][:, 0:T], tokr[xc])
-    for a, k in xpeers:
+        got(spr.at[src], sp_r.at[src])
+
+    ir = iota((64, T), 0).astype(F32)
+
+    def weight_term(src, sel):
+        named = jnp.zeros((64, T), F32)
+        for k in range(K):
+            named += jnp.where(spr[src, 64 + k : 65 + k, 0:T] == ir, sel[k : k + 1, 0:T], 0.0)
+        return dot((spr[src, 0:64, 0:T] + named).astype(BF16), tokr[src])
+
+    wsum = weight_term(xc, selb)
+    for a, k in reversed(xpeers):
         src = m4(x + a) * 2 + lax.rem(c + k, 2)
-        got(lgr.at[src], lg_r.at[src])
-        wsum += dot(lgr[src][:, 0:T], tokr[src])
+        got(selr.at[src], lg_r.at[src])
+        wsum += weight_term(src, selr.at[src])
+    shift = x * 720 - (x * 720) // 128 * 128
+    wsum = pltpu.roll(wsum, lax.rem(BLK - shift, BLK), 1)
     for n in range(16):
-        rss[n] = wsum[4 * n : 4 * n + 4, :]
+        rss[n] = wsum[4 * n : 4 * n + 4, 0:OUT]
+
     chip = y * 4 + z
-    n = 0
-    for a in range(4):
-        for b in range(4):
-            if a or b:
-                dest = m4(y + a) * 4 + m4(z + b)
-                send(rss.at[dest], rsr.at[chip], rs_s.at[n], rs_r.at[chip], at(dy=a, dz=b))
-                n += 1
+    hops = lambda v: min(v[0], 4 - v[0]) + min(v[1], 4 - v[1])
+    for n, (a, b) in enumerate(sorted([(a, b) for a in range(4) for b in range(4) if a or b], key=hops, reverse=True)):
+        dest = m4(y + a) * 4 + m4(z + b)
+        send(rss.at[dest], rsr.at[chip], rs_s.at[n], rs_r.at[chip], at(dy=a, dz=b))
     rsr[chip] = rss[chip]
 
     for a in (1, 2, 3):
@@ -426,10 +441,7 @@
                 src = m4(y + a) * 4 + m4(z + b)
                 got(rsr.at[src], rs_r.at[src])
     out = jnp.sum(rsr[...], axis=0) * (1.0 / math.sqrt(TOTAL))
-    out = jnp.concatenate([out, out], axis=0)
-    shift = x * 720 - (x * 720) // 128 * 128
-    out = pltpu.roll(out, lax.rem(BLK - shift, BLK), 1)
-    wt_o[...] = out[0:4, 0:720]
+    wt_o[...] = out[:, 0:720]
     for s in sent:
         s.wait_send()
 
@@ -445,24 +457,24 @@
         vm((2, ROWS, WIDTH[0]), BF16), vm((2, ROWS, WIDTH[1]), BF16),
         vm((8, ROWS, WIDTH[0]), BF16), vm((8, ROWS, WIDTH[1]), BF16), vm((8, T, BLK), BF16),
         vm((8, E), F32), vm((4, 8, 8, E), F32), vm((K, 256, E), BF16), vm((8, 256), F32), vm((2, 4, 8, 256), F32),
-        vm((2, K, 4 * T), F32), vm((2, K, 8, 4 * T), F32), vm((ROWS, 4 * T), F32), vm((2, 4, 8, 256), F32), vm((2, 4, 8, 256), F32),
+        vm((2, K, 4 * T), F32), vm((2, K, 8, 4 * T), F32), vm((2, 2 * ROWS, 4 * T), F32), vm((2, 4, K, 256), F32), vm((2, 4, K, 256), F32),
         vm((8, E), F32), vm((8, 8, E), F32), vm((4, 8, E), F32), vm((8, E), F32),
         vm((8, E), F32), vm((4, 8, E), F32), vm((8, E), F32), vm((4, 8, E), F32),
-        vm((E, T), F32), vm((E, T), F32), vm((K, T), F32), vm((2, 64, 256), BF16), vm((8, 64, 256), BF16),
-        vm((16, 4, BLK), F32), vm((16, 4, BLK), F32),
-        dma((9,)), dma((2, 2, 3)), dma((2, 2, 3)), dma((2, 2, N)), dma((2, 2, N)), dma((2, 2, N)), dma((2, 2, 2, N)), dma((2, N)), dma((2, 8, N)),
+        vm((E, T), F32), vm((E, T), F32), vm((K, T), F32), vm((2, 72, 256), F32), vm((8, 72, 256), F32),
+        vm((K, 256), F32), vm((8, K, 256), F32), vm((16, 4, OUT), F32), vm((16, 4, OUT), F32), pltpu.SMEM((1,), F32),
+        dma((10,)), dma((2, 2, 3)), dma((2, 2, 3)), dma((2, 2, N)), dma((2, 2, N)), dma((2, 2, N)), dma((2, 2, 2, N)), dma((2, N)), dma((2, 8, N)),
         dma((7,)), dma((8,)), dma((3,)), dma((4,)), dma((2, 3)), dma((2, 4)), dma((7,)), dma((8,)), dma((3,)), dma((4,)),
-        dma((3,)), dma((4,)), dma((3,)), dma((4,)), dma((7,)), dma((8,)), dma((2, 3)), dma((2, 4)), dma((7,)), dma((8,)), dma((15,)), dma((16,)),
+        dma((3,)), dma((4,)), dma((3,)), dma((4,)), dma((7,)), dma((8,)), dma((2, 3)), dma((2, 4)), dma((7,)), dma((8,)), dma((7,)), dma((8,)), dma((15,)), dma((16,)),
     ]
     hbm = pl.BlockSpec(memory_space=pl.ANY)
-    token_grad, weight_grad, loss = pl.pallas_call(
+    logit_grad, weight_grad, loss = pl.pallas_call(
         kernel,
         out_shape=(
-            jax.ShapeDtypeStruct((T, D), BF16),
+            jax.ShapeDtypeStruct((T, E), BF16),
             jax.ShapeDtypeStruct((4, 720), F32),
             jax.ShapeDtypeStruct((1,), F32),
         ),
-        in_specs=[hbm] * 6 + [pl.BlockSpec(memory_space=pltpu.SMEM)],
+        in_specs=[hbm] * 7,
         out_specs=(
             pl.BlockSpec(memory_space=pltpu.VMEM),
             pl.BlockSpec(memory_space=pltpu.VMEM),
@@ -472,6 +484,7 @@
         compiler_params=pltpu.CompilerParams(collective_id=0, has_side_effects=True, vmem_limit_bytes=64000 * 1024),
         name="router",
     )(tokens, out_grad, indices.T, rows, router_weight, router_bias.reshape(1, E), balance_scale)
+    token_grad = dot(logit_grad, router_weight, ((1,), (1,))).astype(BF16)
     return token_grad, weight_grad.T, loss
 
 

time: 87.4 us -> 81.9 us (0.937)
  Pallas kernels: 80.9 us -> 75.7 us
  local copies, waits for them, and re-layouts: 2.94 us -> 0.61 us
  matrix products: 0 us -> 2.27 us
    pallas_call x1, Pallas kernels: 80.9 us -> 75.7 us  [on_device(): pl.pallas_call(kernel, out_shape=(jax.ShapeDtypeStruct((T, E), BF16), jax...]
    unnamed x4 -> x5, local copies, waits for them, and re-layouts: 2.94 us -> 0.61 us
    dot_general x0 -> x1, matrix products: none -> 2.27 us  [dot(): lax.dot_general(a, b, (dims, ((), ())), preferred_element_type=F32, **kw)]
where the time goes in v2:
time: 81.9 us; the launch traced here: 81.7 us
  Pallas kernels  75.7 us (92%)
  between operations  3.13 us (4%)
  matrix products  2.27 us (3%)
    pallas_call x1, Pallas kernels, on_device(): pl.pallas_call(kernel, out_shape=(jax.ShapeDtypeStruct((T, E), BF16), jax...  75.7 us
    dot_general x1, matrix products, dot(): lax.dot_general(a, b, (dims, ((), ())), preferred_element_type=F32, **kw)  2.27 us

profile of v2, /device:TPU:1, one launch (start us, length us, event | category | flops | bytes accessed | tf_op | source)
XLA Modules:
  0.0 81.7 jit_solution(14280027502246761276)
XLA Ops:
  1.3 0.0 copy-start
  1.3 75.7 %router.1 = (bf16[192,128]{1,0:T(8,128)(2,1)}, f32[4,720]{1,0:T(4,128)}, f32[1]{0:T(128)}) custom-call(bf16[192,2880]{1,0:T(8,128)(2,1)} %tok_h.1, bf16[192,2880]{1,0:T(8,128)(2,1)} %og_h.1, s32[4,192]{1,0:T(4,128)} %bitcast.12, bf16[36,32,2880]{2,1,0:T(8,128)(2,1)} %bitcast.10, bf16[2880,128]{1,0:T(8,128)(2,1)} %w_h.1, f32[1,128]{1,0:T(1,128)} %bitcast.13, ...), custom_call_target="tpu_custom_call" | custom-call | tf_op jit(solution)/shard_map/router/pallas_call | solution.py:470
  77.0 0.0 copy-start.1
  77.0 0.0 copy-done
  77.1 2.3 %convolution_convert_fusion = bf16[192,2880]{1,0:T(8,128)(2,1)} fusion(bf16[192,128]{1,0:T(8,128)(2,1)} %get-tuple-element.6, bf16[2880,128]{1,0:T(8,128)(2,1)S(1)} %copy-done), kind=kOutput, calls=%fused_computation | convolution fusion | flops 142110720 | bytes 1892352 | tf_op jit(solution)/shard_map/dot_general | solution.py:32
  79.3 0.0 copy-done.1
  79.3 0.6 copy.13
Async XLA Ops:
  1.3 75.8 %copy-start = (bf16[2880,128]{1,0:T(8,128)(2,1)S(1)}, bf16[2880,128]{1,0:T(8,128)(2,1)}, u32[]{:S(2)}) copy-start(bf16[2880,128]{1,0:T(8,128)(2,1)} %w_h.1) | copy-start | bytes 2211844
  77.0 2.3 %copy-start.1 = (f32[4,720]{1,0:T(4,128)S(1)}, f32[4,720]{1,0:T(4,128)}, u32[]{:S(2)}) copy-start(f32[4,720]{1,0:T(4,128)} %get-tuple-element.7) | copy-start | bytes 34564

commit v3 on v2

--- a/solution.py
+++ b/solution.py
@@ -19,6 +19,7 @@
 WIDTH = (SPLIT, DPAD - SPLIT)
 PER = 27
 ROWS = 112
+MAIN, LAST = 96, 16
 ES = 4 * CAP
 KQ = ES * 8
 PIECES = (((0, 640), (640, 512), (1152, 384)), ((0, 640), (640, 512), (1152, 256)))
@@ -26,6 +27,8 @@
 BLK = 896
 OUT = 768
 TOTAL = 24576
+G_EX, G_OWN, G_OG, G_ME, G_PD = 0, 2, 4, 6, 8
+G_C1, G_C2, G_P1, G_P2, G_XC, G_XP, G_TK, G_SP, G_LG, G_RS = range(10, 20)
 
 
 def dot(a, b, dims=((1,), (0,)), **kw):
@@ -40,16 +43,14 @@
     tok_h, og_h, idx_h, ex_h, w_h, b_h, bs_h,
     lg_o, wt_o, loss_o,
     tokraw, tokp, ogfull, og0, og1, idxv, ev3, ev, wv, bv,
-    snd0, snd1, tr0, tr1, ex0, ex1, tokr,
-    cntsnd, cntr, cc_v, meta, metar, rowsel, acc, gbuf, pds, pdr,
+    snd0, snd1, tr0, tr1, ex0, ex1, exl0, exl1, tokr,
+    cntsnd, cntr, cc_v, meta, metar, rowsel, rowlast, acc, gbuf, pds, pdr,
     psb, psr1, psr2, psb2, xcs, xcr, xps, xpr,
-    lt, pt, mixv, spb, spr, selb, selr, rss, rsr, bs_s,
-    loc, og_s, og_r, ex2_s, ex2_r, fw_s, ex1_s, own_s, exr,
-    c1_s, c1_r, c2_s, c2_r, me_s, me_r, p1_s, p1_r, p2_s, p2_r,
-    xc_s, xc_r, xp_s, xp_r, tk_s, tk_r, pd_s, pd_r, sp_s, sp_r, lg_s, lg_r, rs_s, rs_r,
+    lt, pt, mixv, spb, spr, selb, selr, rss, rsr, bs_s, lgv, wtv, lossv,
+    loc, ss, rr, og_r, ex2_r, exr, last_r, lg_r,
 ):
     y, z, c, x = (lax.axis_index(a) for a in AXES)
-    og, snd, tr, ex = (og0, og1), (snd0, snd1), (tr0, tr1), (ex0, ex1)
+    og, snd, tr, ex, exl = (og0, og1), (snd0, snd1), (tr0, tr1), (ex0, ex1), (exl0, exl1)
     m4 = lambda v: lax.rem(v + 4, 4)
     po = (z, y)
     pe = (y, z)
@@ -64,15 +65,14 @@
     def remote(src, dst, ss, rs, dev):
         return pltpu.make_async_remote_copy(src_ref=src, dst_ref=dst, send_sem=ss, recv_sem=rs, device_id=dev, device_id_type=MESH)
 
-    sent = []
-
-    def send(*a):
-        r = remote(*a)
-        r.start()
-        sent.append(r)
+    def send(src, dst, group, recv, dev):
+        remote(src, dst, ss.at[group], recv, dev).start()
 
     def got(ref, sem):
         remote(ref, ref, sem, sem, at(dx=1)).wait_recv()
+
+    def drain(ref, group):
+        remote(ref, ref, ss.at[group], ss.at[group], at(dx=1)).wait_send()
 
     loads = [
         pltpu.make_async_copy(idx_h, idxv, loc.at[0]),
@@ -114,7 +114,7 @@
             step, same = (ea - pe[h] + 4) % 4, ec == c
             near = jnp.where(step == 1, jnp.where(same, 2, 6), jnp.where(same, 3, 7))
             slot = jnp.where(step == 0, jnp.where(same, 0, 1), jnp.where(step == 2, 4 + ec, near))
-            code = (eb * 1024 + slot * ROWS + po[h] * PER).astype(F32) + off
+            code = (eb * 1024 + slot * 32).astype(F32) + off
             meta[4 * h + k : 4 * h + k + 1, 0:T] = code
 
     loads[1].wait()
@@ -129,27 +129,25 @@
     zpeers = [(b, k) for b in (1, 2, 3) for k in (0, 1)] + [(0, 1)]
     zdev = lambda b, k: at(dz=b, cc=lax.rem(c + k, 2))
     for n, (b, k) in enumerate(zpeers):
-        send(cntsnd, cntr.at[y, zc], c1_s.at[n], c1_r.at[zc], zdev(b, k))
+        send(cntsnd, cntr.at[y, zc], G_C1, rr.at[0], zdev(b, k))
     for h in range(2):
         for s in (1, 2, 3):
-            send(meta, metar.at[h, po[h]], me_s.at[h, s - 1], me_r.at[h, po[h]], og_dev[h](s))
+            send(meta, metar.at[h, po[h]], G_ME + h, rr.at[2 + h], og_dev[h](s))
 
     def og_rows(pos, second):
         return pl.ds(pl.multiple_of(pos * T + second * 96, 32), 96)
 
     def og_send(h, d, m):
         where = og_rows(po[h], d ^ m)
-        send(og[h].at[where, :], og[h].at[where, :], og_s.at[h, d, m], og_r.at[h, d, m], og_dev[h](1 - 2 * d))
+        send(og[h].at[where, :], og[h].at[where, :], G_OG + h, og_r.at[h, 2 if m else d], og_dev[h](1 - 2 * d))
 
     for h in range(2):
         for d in range(2):
             og_send(h, d, 0)
 
-    for b, k in zpeers:
-        src = m4(z + b) * 2 + lax.rem(c + k, 2)
-        got(cntr.at[y, src], c1_r.at[src])
+    got(cntr.at[0, 0:7], rr.at[0])
     for s in (1, 2, 3):
-        send(cntr.at[y], cntr.at[y], c2_s.at[s - 1], c2_r.at[y], at(dy=s))
+        send(cntr.at[y], cntr.at[y], G_C2, rr.at[1], at(dy=s))
     for h in range(2):
         for d in range(2):
             og_send(h, d, 1)
@@ -166,7 +164,7 @@
     xdev = lambda a, k: at(dx=a, cc=lax.rem(c + k, 2))
     tokr[xc] = tokp[:, block(x)]
     for n, (a, k) in enumerate(xpeers):
-        send(tokp.at[:, block(m4(x + a))], tokr.at[xc], tk_s.at[n], tk_r.at[xc], xdev(a, k))
+        send(tokp.at[:, block(m4(x + a))], tokr.at[xc], G_TK, rr.at[4], xdev(a, k))
 
     loads[3].wait()
     loads[4].wait()
@@ -186,7 +184,7 @@
     prow = jnp.sum(jnp.where(diag, pcol, 0.0), axis=0, keepdims=True)
     psb[...] = jnp.broadcast_to(prow, (8, E))
     for n, (b, k) in enumerate(zpeers):
-        send(psb, psr1.at[zc], p1_s.at[n], p1_r.at[zc], zdev(b, k))
+        send(psb, psr1.at[zc], G_P1, rr.at[5], zdev(b, k))
     psr1[zc] = psb[...]
 
     for q in range(4):
@@ -207,17 +205,16 @@
     for h in range(2):
         for d in range(2):
             where = og_rows(og_from(d, h), d)
-            got(og[h].at[where, :], og_r.at[h, d, 0])
-            send(og[h].at[where, :], og[h].at[where, :], og_s.at[h, d, 2], og_r.at[h, d, 2], og_dev[h](1 - 2 * d))
-
-    for s in (1, 2, 3):
-        got(cntr.at[m4(y + s)], c2_r.at[m4(y + s)])
+            got(og[h].at[where, :], og_r.at[h, d])
+            send(og[h].at[where, :], og[h].at[where, :], G_OG + h, og_r.at[h, 2], og_dev[h](1 - 2 * d))
+
+    got(cntr.at[0:3], rr.at[1])
     counts = cntr[...]
     plane = jnp.sum(counts.reshape(32, 8, E), axis=0)
     xcs[...] = plane
     xcr[x] = plane
     for a in (1, 2, 3):
-        send(xcs, xcr.at[x], xc_s.at[a - 1], xc_r.at[x], at(dx=a))
+        send(xcs, xcr.at[x], G_XC, rr.at[7], at(dx=a))
     first = (y * 8 + z * 2 + c) * 4
     cb = counts.reshape(256, E).astype(BF16)
     for k in range(K):
@@ -231,6 +228,8 @@
         rr = row - core * ROWS
         i = jnp.where(rr >= PER, 1, 0) + jnp.where(rr >= 2 * PER, 1, 0) + jnp.where(rr >= 3 * PER, 1, 0)
         r = rr - i * PER
+        i = i + po[h] + 1
+        i = jnp.where(i >= 4, i - 4, i)
         dev = (q * 8 + i * 2 + core) if h == 0 else (i * 8 + q * 2 + core)
         pick = (jnp.broadcast_to(dev[:, 0:1] * 8, (2 * ROWS, 256)) == iota((2 * ROWS, 256), 1))
         pick = jnp.where(pick, 1.0, 0.0).astype(BF16)
@@ -250,16 +249,24 @@
     def core_rows(cc):
         return pl.ds(pl.multiple_of(cc * ROWS, 16), ROWS)
 
-    def cols(h, n):
-        return pl.ds(PIECES[h][n][0], PIECES[h][n][1])
+    def piece(h, ref, row, n):
+        if n == N:
+            return ref.at[pl.ds(pl.multiple_of(row + MAIN, 16), LAST), :]
+        return ref.at[pl.ds(pl.multiple_of(row, 16), MAIN), pl.ds(*PIECES[h][n])]
+
+    def landing(h, slot, n):
+        return exl[h].at[slot] if n == N else ex[h].at[slot, :, pl.ds(*PIECES[h][n])]
+
+    def landed(h, pair, n):
+        return last_r.at[h] if n == N else exr.at[h, pair, n]
 
     for h in range(2):
         gather(h, 2)
         for d in range(2):
-            for n in range(N):
+            for n in range(N + 1):
                 send(
-                    snd[h].at[2, core_rows(d), cols(h, n)], tr[h].at[d, :, cols(h, n)],
-                    ex2_s.at[h, d, n], ex2_r.at[h, d, n], ex_dev[h](1 - 2 * d, c),
+                    piece(h, snd[h].at[2], d * ROWS, n), piece(h, tr[h].at[d], 0, n),
+                    G_EX + h, ex2_r.at[h, d, n], ex_dev[h](1 - 2 * d, c),
                 )
 
     def gather_rest(o, _):
@@ -270,83 +277,89 @@
 
     lax.fori_loop(0, 3, gather_rest, 0)
 
-    def ex1_send(slot):
-        cc = c if slot == 0 else other
-        for n in range(N):
+    def ex1_send(far, pieces):
+        cc = other if far else c
+        for n in pieces:
             for h in range(2):
                 for d in range(2):
+                    slot = 3 - d + 4 * far
                     send(
-                        snd[h].at[1 + 2 * d, core_rows(cc), cols(h, n)], ex[h].at[3 - d + 4 * slot, :, cols(h, n)],
-                        ex1_s.at[h, d, slot, n], exr.at[h, 3 - d + 4 * slot, n], ex_dev[h](1 - 2 * d, cc),
+                        piece(h, snd[h].at[1 + 2 * d], cc * ROWS, n), landing(h, slot, n),
+                        G_EX + h, landed(h, 1 + 2 * far, n), ex_dev[h](1 - 2 * d, cc),
                     )
 
-    ex1_send(0)
-    for h in range(2):
-        for n in range(N):
-            send(
-                snd[h].at[0, core_rows(other), cols(h, n)], ex[h].at[1, :, cols(h, n)],
-                own_s.at[h, n], exr.at[h, 1, n], at(cc=other),
-            )
-        ex[h][0] = snd[h][0, core_rows(c), :]
-
-    for h in range(2):
-        for s in (1, 2, 3):
-            got(metar.at[h, m4(po[h] + s)], me_r.at[h, m4(po[h] + s)])
+    ex1_send(0, range(N))
+    for h in range(2):
+        for n in range(N + 1):
+            send(piece(h, snd[h].at[0], other * ROWS, n), landing(h, 1, n), G_OWN + h, landed(h, 0, n), at(cc=other))
+        ex[h][0] = snd[h][0, pl.ds(pl.multiple_of(c * ROWS, 16), MAIN), :]
+        exl[h][0] = snd[h][0, pl.ds(pl.multiple_of(c * ROWS + MAIN, 16), LAST), :]
+
+    for h in range(2):
+        got(metar.at[h, 0:3], rr.at[2 + h])
         metar[h, po[h]] = meta[...]
         for i in range(4):
-            rowsel[h, :, i * T : (i + 1) * T] = metar[h, i, 4 * h : 4 * h + 4, 0:T] - (pe[1 - h] * 1024).astype(F32)
-        for d in range(2):
-            got(og[h].at[og_rows(og_from(d, h), 1 - d), :], og_r.at[h, d, 1])
-            got(og[h].at[og_rows(m4(po[h] + 2), d), :], og_r.at[h, d, 2])
+            code = metar[h, i, 4 * h : 4 * h + 4, 0:T].astype(I32) - po[h] * 1024
+            slot = code // 32
+            place = code - slot * 32 + m4(i - po[h] - 1) * PER
+            valid = (code >= 0) & (code < 256)
+            rowsel[h, :, i * T : (i + 1) * T] = jnp.where(valid & (place < MAIN), slot * MAIN + place, -1).astype(F32)
+            rowlast[h, i] = jnp.where(valid & (place >= MAIN), slot * LAST + place - MAIN, -1).astype(F32)
+        got(og[h].at[0 : 2 * T, :], og_r.at[h, 2])
     acc[...] = jnp.zeros_like(acc)
 
     def absorb(pair, mine):
         for n in range(N):
             for h in range(2):
-                for slot in (1,) if mine else (0, 1):
-                    got(ex[h].at[2 * pair + slot, :, cols(h, n)], exr.at[h, 2 * pair + slot, n])
+                if mine:
+                    got(landing(h, 1, n), landed(h, 0, n))
+                else:
+                    got(ex[h].at[pl.ds(2 * pair, 2), :, pl.ds(*PIECES[h][n])], landed(h, pair, n))
                 lo, w = PIECES[h][n]
-                block = ex[h][pl.ds(2 * pair, 2), :, lo : lo + w].reshape(2 * ROWS, w)
+                block = ex[h][pl.ds(2 * pair, 2), :, lo : lo + w].reshape(2 * MAIN, w)
                 part = dot(block, og[h][:, lo : lo + w], ((1,), (1,)))
                 if n == 0:
                     gbuf[h] = part
                 else:
                     gbuf[h] += part
-        rid = (iota((2 * ROWS, 128), 0) + pair * 2 * ROWS).astype(F32)
+        rid = (iota((2 * MAIN, 128), 0) + pair * 2 * MAIN).astype(F32)
         for h in range(2):
             for lb in range(6):
                 lanes = slice(lb * 128, lb * 128 + 128)
                 g = gbuf[h, :, lanes]
                 for k in range(K):
                     hit = jnp.where(rid == rowsel[h, k : k + 1, lanes], g, 0.0)
-                    acc[h, k, :, lanes] += jnp.sum(hit.reshape(2 * ROWS // 8, 8, 128), axis=0)
+                    acc[h, k, :, lanes] += jnp.sum(hit.reshape(2 * MAIN // 8, 8, 128), axis=0)
 
     absorb(0, True)
 
-    for n in range(N):
+    def forward(n):
         for h in range(2):
             for d in range(2):
-                got(tr[h].at[d, :, cols(h, n)], ex2_r.at[h, d, n])
+                got(piece(h, tr[h].at[d], 0, n), ex2_r.at[h, d, n])
                 send(
-                    tr[h].at[d, :, cols(h, n)], ex[h].at[4 + c, :, cols(h, n)],
-                    fw_s.at[h, d, n], exr.at[h, 4 + c, n], ex_dev[h](1 - 2 * d, d),
+                    piece(h, tr[h].at[d], 0, n), landing(h, 4 + c, n),
+                    G_EX + h, landed(h, 2, n), ex_dev[h](1 - 2 * d, d),
                 )
-    ex1_send(1)
-
-    for b, k in zpeers:
-        src = m4(z + b) * 2 + lax.rem(c + k, 2)
-        got(psr1.at[src], p1_r.at[src])
+
+    for n in range(N):
+        forward(n)
+    ex1_send(1, range(N))
+    forward(N)
+    for far in range(2):
+        ex1_send(far, (N,))
+
+    got(psr1.at[0:7], rr.at[5])
     psb2[...] = jnp.sum(psr1[...], axis=0)
     psr2[y] = psb2[...]
     for s in (1, 2, 3):
-        send(psb2, psr2.at[y], p2_s.at[s - 1], p2_r.at[y], at(dy=s))
-
-    for a in (1, 2, 3):
-        got(xcr.at[m4(x + a)], xc_r.at[m4(x + a)])
+        send(psb2, psr2.at[y], G_P2, rr.at[6], at(dy=s))
+
+    got(xcr.at[0:3], rr.at[7])
     cnt_row = jnp.sum(xcr[...], axis=0)[0:1, :]
     cnt_col = jnp.sum(jnp.where(diag, cnt_row, 0.0), axis=1, keepdims=True)
     loads[9].wait()
-    push = bs_s[0] * E * (cnt_col / (TOTAL * K))
+    push = bs_s[...] * E * (cnt_col / (TOTAL * K))
     prob = pt[...]
     spread = prob * (push - jnp.sum(prob * push, axis=0, keepdims=True))
     lt[...] = spread
@@ -358,7 +371,7 @@
             ik = idxv[k : k + 1, :]
             spb[par, 64 + k : 65 + k, 0:T] = jnp.where((ik // 4) % 2 == par, ik // 8 * 4 + ik % 4, -1).astype(F32)
     for n, (a, k) in enumerate(xpeers):
-        send(spb.at[lax.rem(c + k, 2)], spr.at[xc], sp_s.at[n], sp_r.at[xc], xdev(a, k))
+        send(spb.at[lax.rem(c + k, 2)], spr.at[xc], G_SP, rr.at[9], xdev(a, k))
     spr[xc] = spb[c]
 
     def arrivals(pair, _):
@@ -373,37 +386,44 @@
             for k in range(K):
                 pds[h, i, k : k + 1, 0:T] = jnp.sum(acc[h, k, :, i * T : (i + 1) * T], axis=0, keepdims=True)
         for s in (1, 2, 3):
-            send(pds.at[h, m4(po[h] + s)], pdr.at[h, po[h]], pd_s.at[h, s - 1], pd_r.at[h, po[h]], og_dev[h](s))
+            send(pds.at[h, m4(po[h] + s)], pdr.at[h, po[h]], G_PD + h, rr.at[10 + h], og_dev[h](s))
         pdr[h, po[h]] = pds[h, po[h]]
-    for s in (1, 2, 3):
-        got(psr2.at[m4(y + s)], p2_r.at[m4(y + s)])
+    got(psr2.at[0:3], rr.at[6])
     xps[...] = jnp.sum(psr2[...], axis=0)
     xpr[x] = xps[...]
     for a in (1, 2, 3):
-        send(xps, xpr.at[x], xp_s.at[a - 1], xp_r.at[x], at(dx=a))
+        send(xps, xpr.at[x], G_XP, rr.at[8], at(dx=a))
+    late = [jnp.zeros((1, T), F32)] * K
+    rid = iota((8 * LAST, T), 0).astype(F32)
+    for h in range(2):
+        got(exl[h].at[1:8], last_r.at[h])
+        g = dot(exl[h][...].reshape(8 * LAST, WIDTH[h]), og[h][own_og[h], :], ((1,), (1,)))
+        for k in range(K):
+            hit = jnp.where(rid == rowlast[h, po[h], k : k + 1, :], g, 0.0)
+            late[k] += jnp.sum(hit, axis=0, keepdims=True)
+
     pd = jnp.zeros((K, 256), F32)
     for h in range(2):
-        for s in (1, 2, 3):
-            got(pdr.at[h, m4(po[h] + s)], pd_r.at[h, m4(po[h] + s)])
+        got(pdr.at[h, 0:3], rr.at[10 + h])
         pd += (pdr[h, 0] + pdr[h, 1]) + (pdr[h, 2] + pdr[h, 3])
 
-    dots = [pd[k : k + 1, 0:T] for k in range(K)]
+    dots = [pd[k : k + 1, 0:T] + late[k] for k in range(K)]
     mix = [mixv[k : k + 1, :] for k in range(K)]
     mean = mix[0] * dots[0] + mix[1] * dots[1] + mix[2] * dots[2] + mix[3] * dots[3]
     for k in range(K):
         selb[k : k + 1, 0:T] = mix[k] * (dots[k] - mean)
     selb[:, T:256] = jnp.zeros((K, 256 - T), F32)
     for n, (a, k) in enumerate(xpeers):
-        send(selb, selr.at[xc], lg_s.at[n], lg_r.at[xc], xdev(a, k))
+        send(selb, selr.at[xc], G_LG, lg_r.at[xc], xdev(a, k))
 
     lg = jnp.zeros((E, T), F32)
     for k in range(K):
         lg += jnp.where(idxv[k : k + 1, :] == ie, selb[k : k + 1, 0:T], 0.0)
-    lg_o[...] = jnp.transpose(lt[...] + lg).astype(BF16)
-    for a, k in xpeers:
-        src = m4(x + a) * 2 + lax.rem(c + k, 2)
-        got(tokr.at[src], tk_r.at[src])
-        got(spr.at[src], sp_r.at[src])
+    lgv[...] = jnp.transpose(lt[...] + lg).astype(BF16)
+    out_lg = pltpu.make_async_copy(lgv, lg_o, loc.at[10])
+    out_lg.start()
+    got(tokr.at[0:7], rr.at[4])
+    got(spr.at[0:7], rr.at[9])
 
     ir = iota((64, T), 0).astype(F32)
 
@@ -427,23 +447,53 @@
     hops = lambda v: min(v[0], 4 - v[0]) + min(v[1], 4 - v[1])
     for n, (a, b) in enumerate(sorted([(a, b) for a in range(4) for b in range(4) if a or b], key=hops, reverse=True)):
         dest = m4(y + a) * 4 + m4(z + b)
-        send(rss.at[dest], rsr.at[chip], rs_s.at[n], rs_r.at[chip], at(dy=a, dz=b))
+        send(rss.at[dest], rsr.at[chip], G_RS, rr.at[12], at(dy=a, dz=b))
     rsr[chip] = rss[chip]
 
-    for a in (1, 2, 3):
-        got(xpr.at[m4(x + a)], xp_r.at[m4(x + a)])
+    got(xpr.at[0:3], rr.at[8])
     ps_row = jnp.sum(xpr[...], axis=0)[0:1, :]
-    loss_o[0] = E * jnp.sum((cnt_row / (TOTAL * K)) * (ps_row / TOTAL))
-
-    for a in range(4):
-        for b in range(4):
-            if a or b:
-                src = m4(y + a) * 4 + m4(z + b)
-                got(rsr.at[src], rs_r.at[src])
+    lossv[0] = E * jnp.sum((cnt_row / (TOTAL * K)) * (ps_row / TOTAL))
+
+    out_loss = pltpu.make_async_copy(lossv, loss_o, loc.at[11])
+    out_loss.start()
+    for h in range(2):
+        drain(snd[h], G_EX + h)
+        drain(snd[h].at[0, 0:ROWS, :], G_OWN + h)
+        drain(og[h].at[0 : 3 * T, :], G_OG + h)
+        drain(metar.at[h, 0:3], G_ME + h)
+        drain(pdr.at[h, 0:3], G_PD + h)
+    for ref, group in (
+        (cntr.at[0, 0:7], G_C1), (cntr.at[0:3], G_C2), (psr1.at[0:7], G_P1), (psr2.at[0:3], G_P2), (xcr.at[0:3], G_XC), (xpr.at[0:3], G_XP),
+        (tokr.at[0:7], G_TK), (spr.at[0:7], G_SP), (selr.at[0:7], G_LG), (rsr.at[0:15], G_RS),
+    ):
+        drain(ref, group)
+    out_lg.wait()
+    got(rsr.at[0:15], rr.at[12])
     out = jnp.sum(rsr[...], axis=0) * (1.0 / math.sqrt(TOTAL))
-    wt_o[...] = out[:, 0:720]
-    for s in sent:
-        s.wait_send()
+    wtv[...] = out[:, 0:720]
+    out_wt = pltpu.make_async_copy(wtv, wt_o, loc.at[12])
+    out_wt.start()
+    out_loss.wait()
+    out_wt.wait()
+
+
+def finish(lg_h, w_h, wt_h, loss_h, tg_o, wt_o, loss_o, lgv, wv, tgv, sem):
+    lg_in = pltpu.make_async_copy(lg_h, lgv, sem.at[0])
+    lg_in.start()
+    w_in = pltpu.make_async_copy(w_h, wv, sem.at[5])
+    w_in.start()
+    moves = [pltpu.make_async_copy(wt_h, wt_o, sem.at[1]), pltpu.make_async_copy(loss_h, loss_o, sem.at[2])]
+    for m in moves:
+        m.start()
+    lg_in.wait()
+    w_in.wait()
+    for n in range(2):
+        rows = pl.ds(n * 96, 96)
+        tgv[rows, :] = dot(lgv[rows, :], wv[...], ((1,), (1,))).astype(BF16)
+        moves.append(pltpu.make_async_copy(tgv.at[rows, :], tg_o.at[rows, :], sem.at[3 + n]))
+        moves[-1].start()
+    for m in moves:
+        m.wait()
 
 
 def on_device(tokens, out_grad, indices, expert_rows, router_weight, router_bias, balance_scale):
@@ -455,18 +505,17 @@
         vm((K, T), I32), vm((4, ES, 8, D), BF16), vm((4 * KQ, DPAD), BF16), vm((D, E), BF16), vm((1, E), F32),
         vm((4, 2 * ROWS, WIDTH[0]), BF16), vm((4, 2 * ROWS, WIDTH[1]), BF16),
         vm((2, ROWS, WIDTH[0]), BF16), vm((2, ROWS, WIDTH[1]), BF16),
-        vm((8, ROWS, WIDTH[0]), BF16), vm((8, ROWS, WIDTH[1]), BF16), vm((8, T, BLK), BF16),
+        vm((8, MAIN, WIDTH[0]), BF16), vm((8, MAIN, WIDTH[1]), BF16), vm((8, LAST, WIDTH[0]), BF16), vm((8, LAST, WIDTH[1]), BF16),
+        vm((8, T, BLK), BF16),
         vm((8, E), F32), vm((4, 8, 8, E), F32), vm((K, 256, E), BF16), vm((8, 256), F32), vm((2, 4, 8, 256), F32),
-        vm((2, K, 4 * T), F32), vm((2, K, 8, 4 * T), F32), vm((2, 2 * ROWS, 4 * T), F32), vm((2, 4, K, 256), F32), vm((2, 4, K, 256), F32),
+        vm((2, K, 4 * T), F32), vm((2, 4, K, T), F32), vm((2, K, 8, 4 * T), F32), vm((2, 2 * MAIN, 4 * T), F32), vm((2, 4, K, 256), F32), vm((2, 4, K, 256), F32),
         vm((8, E), F32), vm((8, 8, E), F32), vm((4, 8, E), F32), vm((8, E), F32),
         vm((8, E), F32), vm((4, 8, E), F32), vm((8, E), F32), vm((4, 8, E), F32),
         vm((E, T), F32), vm((E, T), F32), vm((K, T), F32), vm((2, 72, 256), F32), vm((8, 72, 256), F32),
-        vm((K, 256), F32), vm((8, K, 256), F32), vm((16, 4, OUT), F32), vm((16, 4, OUT), F32), pltpu.SMEM((1,), F32),
-        dma((10,)), dma((2, 2, 3)), dma((2, 2, 3)), dma((2, 2, N)), dma((2, 2, N)), dma((2, 2, N)), dma((2, 2, 2, N)), dma((2, N)), dma((2, 8, N)),
-        dma((7,)), dma((8,)), dma((3,)), dma((4,)), dma((2, 3)), dma((2, 4)), dma((7,)), dma((8,)), dma((3,)), dma((4,)),
-        dma((3,)), dma((4,)), dma((3,)), dma((4,)), dma((7,)), dma((8,)), dma((2, 3)), dma((2, 4)), dma((7,)), dma((8,)), dma((7,)), dma((8,)), dma((15,)), dma((16,)),
+        vm((K, 256), F32), vm((8, K, 256), F32), vm((16, 4, OUT), F32), vm((16, 4, OUT), F32), vm((1, 1), F32), vm((T, E), BF16), vm((4, 720), F32), pltpu.SMEM((1,), F32),
+        dma((13,)), dma((20,)), dma((13,)), dma((2, 3)), dma((2, 2, N + 1)), dma((2, 4, N)), dma((2,)), dma((8,)),
     ]
-    hbm = pl.BlockSpec(memory_space=pl.ANY)
+    hbm = pl.BlockSpec(memory_space=pltpu.HBM)
     logit_grad, weight_grad, loss = pl.pallas_call(
         kernel,
         out_shape=(
@@ -475,16 +524,23 @@
             jax.ShapeDtypeStruct((1,), F32),
         ),
         in_specs=[hbm] * 7,
-        out_specs=(
-            pl.BlockSpec(memory_space=pltpu.VMEM),
-            pl.BlockSpec(memory_space=pltpu.VMEM),
-            pl.BlockSpec(memory_space=pltpu.SMEM),
-        ),
+        out_specs=(hbm, hbm, hbm),
         scratch_shapes=scratch,
         compiler_params=pltpu.CompilerParams(collective_id=0, has_side_effects=True, vmem_limit_bytes=64000 * 1024),
         name="router",
-    )(tokens, out_grad, indices.T, rows, router_weight, router_bias.reshape(1, E), balance_scale)
-    token_grad = dot(logit_grad, router_weight, ((1,), (1,))).astype(BF16)
+    )(tokens, out_grad, indices.T, rows, router_weight, router_bias.reshape(1, E), balance_scale.reshape(1, 1))
+    token_grad, weight_grad, loss = pl.pallas_call(
+        finish,
+        out_shape=(
+            jax.ShapeDtypeStruct((T, D), BF16),
+            jax.ShapeDtypeStruct((4, 720), F32),
+            jax.ShapeDtypeStruct((1,), F32),
+        ),
+        in_specs=[hbm] * 4,
+        out_specs=(hbm, hbm, hbm),
+        scratch_shapes=[vm((T, E), BF16), vm((D, E), BF16), vm((T, D), BF16), dma((6,))],
+        name="finish",
+    )(logit_grad, router_weight, weight_grad, loss)
     return token_grad, weight_grad.T, loss
 
 

time: 81.9 us -> 75.5 us (0.922)
  matrix products: 2.27 us -> 0 us
  between operations: 3.13 us -> 1.29 us
  Pallas kernels: 75.7 us -> 74.1 us
    pallas_call x1, Pallas kernels: 75.7 us -> 70.9 us  [on_device(): pl.pallas_call(kernel, out_shape=(jax.ShapeDtypeStruct((T, E), BF16), jax...]
    pallas_call x0 -> x1, Pallas kernels: none -> 3.17 us  [on_device(): pl.pallas_call(finish, out_shape=(jax.ShapeDtypeStruct((T, D), BF16), jax...]
    dot_general x1 -> x0, matrix products: 2.27 us -> none  [dot(): lax.dot_general(a, b, (dims, ((), ())), preferred_element_type=F32, **kw)]
where the time goes in v3:
time: 75.5 us; the launch traced here: 75.4 us
  Pallas kernels  74.1 us (98%)
  between operations  1.29 us (2%)
    pallas_call x1, Pallas kernels, on_device(): pl.pallas_call(kernel, out_shape=(jax.ShapeDtypeStruct((T, E), BF16), jax...  70.9 us
    pallas_call x1, Pallas kernels, on_device(): pl.pallas_call(finish, out_shape=(jax.ShapeDtypeStruct((T, D), BF16), jax...  3.17 us

profile of v3, /device:TPU:1, one launch (start us, length us, event | category | flops | bytes accessed | tf_op | source)
XLA Modules:
  0.0 75.4 jit_solution(14885181068434645749)
XLA Ops:
  1.3 70.9 %router.1 = (bf16[192,128]{1,0:T(8,128)(2,1)}, f32[4,720]{1,0:T(4,128)}, f32[1]{0:T(128)}) custom-call(bf16[192,2880]{1,0:T(8,128)(2,1)} %tok_h.1, bf16[192,2880]{1,0:T(8,128)(2,1)} %og_h.1, s32[4,192]{1,0:T(4,128)} %bitcast.11, bf16[36,32,2880]{2,1,0:T(8,128)(2,1)} %bitcast.10, bf16[2880,128]{1,0:T(8,128)(2,1)} %w_h.3, f32[1,128]{1,0:T(1,128)} %bitcast.12, ...), custom_call_target="tpu_custom_call" | custom-call | tf_op jit(solution)/shard_map/router/pallas_call | solution.py:519
  72.2 3.2 %finish.1 = (bf16[192,2880]{1,0:T(8,128)(2,1)}, f32[4,720]{1,0:T(4,128)}, f32[1]{0:T(128)}) custom-call(bf16[192,128]{1,0:T(8,128)(2,1)} %get-tuple-element.9.lg_h, bf16[2880,128]{1,0:T(8,128)(2,1)} %w_h.3, f32[4,720]{1,0:T(4,128)} %get-tuple-element.10.wt_h, f32[1]{0:T(128)} %get-tuple-element.11.loss_h), custom_call_target="tpu_custom_call" | custom-call | tf_op jit(solution)/shard_map/finish/pallas_call | solution.py:532

commit v4 on v3

--- a/solution.py
+++ b/solution.py
@@ -40,13 +40,13 @@
 
 
 def kernel(
-    tok_h, og_h, idx_h, ex_h, w_h, b_h, bs_h,
-    lg_o, wt_o, loss_o,
+    tok_h, og_h, idx_h, ex_h, w_h, b_h, bs_s,
+    tg_o, small_o,
     tokraw, tokp, ogfull, og0, og1, idxv, ev3, ev, wv, bv,
     snd0, snd1, tr0, tr1, ex0, ex1, exl0, exl1, tokr,
     cntsnd, cntr, cc_v, meta, metar, rowsel, rowlast, acc, gbuf, pds, pdr,
     psb, psr1, psr2, psb2, xcs, xcr, xps, xpr,
-    lt, pt, mixv, spb, spr, selb, selr, rss, rsr, bs_s, lgv, wtv, lossv,
+    lt, pt, mixv, spb, spr, selb, selr, rss, rsr, lgv,
     loc, ss, rr, og_r, ex2_r, exr, last_r, lg_r,
 ):
     y, z, c, x = (lax.axis_index(a) for a in AXES)
@@ -81,7 +81,6 @@
         pltpu.make_async_copy(w_h, wv, loc.at[3]),
         pltpu.make_async_copy(b_h, bv, loc.at[4]),
     ] + [pltpu.make_async_copy(ex_h.at[:, q * 8 : q * 8 + 8, :], ev3.at[q], loc.at[5 + q]) for q in range(4)]
-    loads.append(pltpu.make_async_copy(bs_h, bs_s, loc.at[9]))
     for l in loads:
         l.start()
     peers = [at(dy=a, dz=b) for a in range(4) for b in range(4) if a or b]
@@ -358,8 +357,7 @@
     got(xcr.at[0:3], rr.at[7])
     cnt_row = jnp.sum(xcr[...], axis=0)[0:1, :]
     cnt_col = jnp.sum(jnp.where(diag, cnt_row, 0.0), axis=1, keepdims=True)
-    loads[9].wait()
-    push = bs_s[...] * E * (cnt_col / (TOTAL * K))
+    push = bs_s[0] * E * (cnt_col / (TOTAL * K))
     prob = pt[...]
     spread = prob * (push - jnp.sum(prob * push, axis=0, keepdims=True))
     lt[...] = spread
@@ -397,7 +395,9 @@
     rid = iota((8 * LAST, T), 0).astype(F32)
     for h in range(2):
         got(exl[h].at[1:8], last_r.at[h])
-        g = dot(exl[h][...].reshape(8 * LAST, WIDTH[h]), og[h][own_og[h], :], ((1,), (1,)))
+    both = [dot(exl[h][...].reshape(8 * LAST, WIDTH[h]), og[h][own_og[h], :], ((1,), (1,))) for h in range(2)]
+    for h in range(2):
+        g = both[h]
         for k in range(K):
             hit = jnp.where(rid == rowlast[h, po[h], k : k + 1, :], g, 0.0)
             late[k] += jnp.sum(hit, axis=0, keepdims=True)
@@ -420,8 +420,6 @@
     for k in range(K):
         lg += jnp.where(idxv[k : k + 1, :] == ie, selb[k : k + 1, 0:T], 0.0)
     lgv[...] = jnp.transpose(lt[...] + lg).astype(BF16)
-    out_lg = pltpu.make_async_copy(lgv, lg_o, loc.at[10])
-    out_lg.start()
     got(tokr.at[0:7], rr.at[4])
     got(spr.at[0:7], rr.at[9])
 
@@ -449,13 +447,13 @@
         dest = m4(y + a) * 4 + m4(z + b)
         send(rss.at[dest], rsr.at[chip], G_RS, rr.at[12], at(dy=a, dz=b))
     rsr[chip] = rss[chip]
+    tg_o[...] = dot(lgv[...], wv[...], ((1,), (1,))).astype(BF16)
 
     got(xpr.at[0:3], rr.at[8])
     ps_row = jnp.sum(xpr[...], axis=0)[0:1, :]
-    lossv[0] = E * jnp.sum((cnt_row / (TOTAL * K)) * (ps_row / TOTAL))
-
-    out_loss = pltpu.make_async_copy(lossv, loss_o, loc.at[11])
-    out_loss.start()
+    loss = E * jnp.sum((cnt_row / (TOTAL * K)) * (ps_row / TOTAL), axis=1, keepdims=True)
+    small_o[4:8, :] = jnp.broadcast_to(loss, (4, OUT))
+
     for h in range(2):
         drain(snd[h], G_EX + h)
         drain(snd[h].at[0, 0:ROWS, :], G_OWN + h)
@@ -467,33 +465,23 @@
         (tokr.at[0:7], G_TK), (spr.at[0:7], G_SP), (selr.at[0:7], G_LG), (rsr.at[0:15], G_RS),
     ):
         drain(ref, group)
-    out_lg.wait()
     got(rsr.at[0:15], rr.at[12])
     out = jnp.sum(rsr[...], axis=0) * (1.0 / math.sqrt(TOTAL))
-    wtv[...] = out[:, 0:720]
-    out_wt = pltpu.make_async_copy(wtv, wt_o, loc.at[12])
-    out_wt.start()
-    out_loss.wait()
-    out_wt.wait()
-
-
-def finish(lg_h, w_h, wt_h, loss_h, tg_o, wt_o, loss_o, lgv, wv, tgv, sem):
-    lg_in = pltpu.make_async_copy(lg_h, lgv, sem.at[0])
-    lg_in.start()
-    w_in = pltpu.make_async_copy(w_h, wv, sem.at[5])
-    w_in.start()
-    moves = [pltpu.make_async_copy(wt_h, wt_o, sem.at[1]), pltpu.make_async_copy(loss_h, loss_o, sem.at[2])]
-    for m in moves:
-        m.start()
-    lg_in.wait()
-    w_in.wait()
-    for n in range(2):
-        rows = pl.ds(n * 96, 96)
-        tgv[rows, :] = dot(lgv[rows, :], wv[...], ((1,), (1,))).astype(BF16)
-        moves.append(pltpu.make_async_copy(tgv.at[rows, :], tg_o.at[rows, :], sem.at[3 + n]))
-        moves[-1].start()
-    for m in moves:
-        m.wait()
+    small_o[0:4, :] = out[:, 0:OUT]
+
+
+def finish(tg_ref, small_ref, tg_o, wt_o, loss_o, wtv, lossv, sem):
+    tg_out = pltpu.make_async_copy(tg_ref, tg_o, sem.at[0])
+    tg_out.start()
+    wtv[...] = small_ref[0:4, 0:720]
+    wt_out = pltpu.make_async_copy(wtv, wt_o, sem.at[1])
+    wt_out.start()
+    lossv[0] = jnp.sum(small_ref[4:5, 0:1])
+    loss_out = pltpu.make_async_copy(lossv, loss_o, sem.at[2])
+    loss_out.start()
+    loss_out.wait()
+    tg_out.wait()
+    wt_out.wait()
 
 
 def on_device(tokens, out_grad, indices, expert_rows, router_weight, router_bias, balance_scale):
@@ -512,23 +500,26 @@
         vm((8, E), F32), vm((8, 8, E), F32), vm((4, 8, E), F32), vm((8, E), F32),
         vm((8, E), F32), vm((4, 8, E), F32), vm((8, E), F32), vm((4, 8, E), F32),
         vm((E, T), F32), vm((E, T), F32), vm((K, T), F32), vm((2, 72, 256), F32), vm((8, 72, 256), F32),
-        vm((K, 256), F32), vm((8, K, 256), F32), vm((16, 4, OUT), F32), vm((16, 4, OUT), F32), vm((1, 1), F32), vm((T, E), BF16), vm((4, 720), F32), pltpu.SMEM((1,), F32),
-        dma((13,)), dma((20,)), dma((13,)), dma((2, 3)), dma((2, 2, N + 1)), dma((2, 4, N)), dma((2,)), dma((8,)),
+        vm((K, 256), F32), vm((8, K, 256), F32), vm((16, 4, OUT), F32), vm((16, 4, OUT), F32), vm((T, E), BF16),
+        dma((9,)), dma((20,)), dma((13,)), dma((2, 3)), dma((2, 2, N + 1)), dma((2, 4, N)), dma((2,)), dma((8,)),
     ]
     hbm = pl.BlockSpec(memory_space=pltpu.HBM)
-    logit_grad, weight_grad, loss = pl.pallas_call(
+    in_vmem = pl.BlockSpec(memory_space=vm)
+    token_grad, small = pl.pallas_call(
         kernel,
-        out_shape=(
-            jax.ShapeDtypeStruct((T, E), BF16),
-            jax.ShapeDtypeStruct((4, 720), F32),
-            jax.ShapeDtypeStruct((1,), F32),
+        out_shape=(vm((T, D), BF16), vm((8, OUT), F32)),
+        in_specs=[hbm] * 6 + [pl.BlockSpec(memory_space=pltpu.SMEM)],
+        out_specs=(in_vmem, in_vmem),
+        scratch_shapes=scratch,
+        compiler_params=pltpu.CompilerParams(collective_id=0, has_side_effects=True, vmem_limit_bytes=54000 * 1024),
+        name="router",
+    )(
+        *(
+            pltpu.with_memory_space_constraint(a, pltpu.HBM)
+            for a in (tokens, out_grad, indices.T, rows, router_weight, router_bias.reshape(1, E))
         ),
-        in_specs=[hbm] * 7,
-        out_specs=(hbm, hbm, hbm),
-        scratch_shapes=scratch,
-        compiler_params=pltpu.CompilerParams(collective_id=0, has_side_effects=True, vmem_limit_bytes=64000 * 1024),
-        name="router",
-    )(tokens, out_grad, indices.T, rows, router_weight, router_bias.reshape(1, E), balance_scale.reshape(1, 1))
+        balance_scale,
+    )
     token_grad, weight_grad, loss = pl.pallas_call(
         finish,
         out_shape=(
@@ -536,11 +527,11 @@
             jax.ShapeDtypeStruct((4, 720), F32),
             jax.ShapeDtypeStruct((1,), F32),
         ),
-        in_specs=[hbm] * 4,
+        in_specs=[in_vmem] * 2,
         out_specs=(hbm, hbm, hbm),
-        scratch_shapes=[vm((T, E), BF16), vm((D, E), BF16), vm((T, D), BF16), dma((6,))],
+        scratch_shapes=[vm((4, 720), F32), pltpu.SMEM((1,), F32), dma((3,))],
         name="finish",
-    )(logit_grad, router_weight, weight_grad, loss)
+    )(*(pltpu.with_memory_space_constraint(a, vm) for a in (token_grad, small)))
     return token_grad, weight_grad.T, loss
 
 

time: 75.5 us -> 72.6 us (0.962)
  Pallas kernels: 74.1 us -> 71.2 us
    pallas_call x1, Pallas kernels: 3.17 us -> 1.03 us  [on_device(): pl.pallas_call(finish, out_shape=(jax.ShapeDtypeStruct((T, D), BF16), jax...]
where the time goes in v4:
time: 72.6 us; the launch traced here: 72.5 us
  Pallas kernels  71.2 us (98%)
  between operations  1.29 us (2%)
    pallas_call x1, Pallas kernels, on_device(): pl.pallas_call(kernel, out_shape=(vm((T, D), BF16), vm((8, OUT), F32)), i...  70.2 us

profile of v4, /device:TPU:1, one launch (start us, length us, event | category | flops | bytes accessed | tf_op | source)
XLA Modules:
  0.0 72.5 jit_solution(108295552739603618)
XLA Ops:
  1.3 70.2 %router.1 = (bf16[192,2880]{1,0:T(8,128)(2,1)S(1)}, f32[8,768]{1,0:T(8,128)S(1)}) custom-call(bf16[192,2880]{1,0:T(8,128)(2,1)} %tok_h.1, bf16[192,2880]{1,0:T(8,128)(2,1)} %og_h.1, s32[4,192]{1,0:T(4,128)} %bitcast.9, bf16[36,32,2880]{2,1,0:T(8,128)(2,1)} %bitcast.8, bf16[2880,128]{1,0:T(8,128)(2,1)} %w_h.1, f32[1,128]{1,0:T(1,128)} %bitcast.10, ...), custom_call_target="tpu_custom_call" | custom-call | tf_op jit(solution)/shard_map/router/pallas_call | solution.py:508
  71.4 1.0 %finish.1 = (bf16[192,2880]{1,0:T(8,128)(2,1)}, f32[4,720]{1,0:T(4,128)}, f32[1]{0:T(128)}) custom-call(bf16[192,2880]{1,0:T(8,128)(2,1)S(1)} %get-tuple-element.8.tg_ref, f32[8,768]{1,0:T(8,128)S(1)} %get-tuple-element.9.small_ref), custom_call_target="tpu_custom_call" | custom-call | tf_op jit(solution)/shard_map/finish/pallas_call | solution.py:523

commit v5 on v4

--- a/solution.py
+++ b/solution.py
@@ -15,20 +15,22 @@
 
 D, E, T, K, CAP = 2880, 128, 192, 4, 9
 DPAD = 2944
-SPLIT = 1536
-WIDTH = (SPLIT, DPAD - SPLIT)
+SPLIT = 1408
+FIRST, WIDTH = (SPLIT, 0), (DPAD - SPLIT, SPLIT)
 PER = 27
 ROWS = 112
 MAIN, LAST = 96, 16
 ES = 4 * CAP
 KQ = ES * 8
-PIECES = (((0, 640), (640, 512), (1152, 384)), ((0, 640), (640, 512), (1152, 256)))
+PIECES = ((0, 640), (640, 512), (1152, 256))
 N = 3
+HALF = MAIN // 2
 BLK = 896
 OUT = 768
 TOTAL = 24576
 G_EX, G_OWN, G_OG, G_ME, G_PD = 0, 2, 4, 6, 8
 G_C1, G_C2, G_P1, G_P2, G_XC, G_XP, G_TK, G_SP, G_LG, G_RS = range(10, 20)
+G_TL, G_TO, G_LS, G_OL = 20, 21, 22, 24
 
 
 def dot(a, b, dims=((1,), (0,)), **kw):
@@ -43,11 +45,11 @@
     tok_h, og_h, idx_h, ex_h, w_h, b_h, bs_s,
     tg_o, small_o,
     tokraw, tokp, ogfull, og0, og1, idxv, ev3, ev, wv, bv,
-    snd0, snd1, tr0, tr1, ex0, ex1, exl0, exl1, tokr,
+    snd0, snd1, tr0, tr1, ex0, ex1, exl0, exl1, tls, trt, ext, ogr, tokr,
     cntsnd, cntr, cc_v, meta, metar, rowsel, rowlast, acc, gbuf, pds, pdr,
     psb, psr1, psr2, psb2, xcs, xcr, xps, xpr,
     lt, pt, mixv, spb, spr, selb, selr, rss, rsr, lgv,
-    loc, ss, rr, og_r, ex2_r, exr, last_r, lg_r,
+    loc, ss, rr, og_r, ex2_r, exr, last_r, tr_r, tail_r, lg_r,
 ):
     y, z, c, x = (lax.axis_index(a) for a in AXES)
     og, snd, tr, ex, exl = (og0, og1), (snd0, snd1), (tr0, tr1), (ex0, ex1), (exl0, exl1)
@@ -118,9 +120,9 @@
 
     loads[1].wait()
     own_og = [pl.ds(pl.multiple_of(po[h] * T, T), T) for h in range(2)]
-    og0[own_og[0], :] = ogfull[:, 0:SPLIT]
-    og1[own_og[1], WIDTH[1] - 128 : WIDTH[1]] = jnp.zeros((T, 128), BF16)
-    og1[own_og[1], 0 : D - SPLIT] = ogfull[:, SPLIT:D]
+    og0[own_og[0], WIDTH[0] - 128 : WIDTH[0]] = jnp.zeros((T, 128), BF16)
+    og0[own_og[0], 0 : D - SPLIT] = ogfull[:, SPLIT:D]
+    og1[own_og[1], :] = ogfull[:, 0:SPLIT]
     pl.semaphore_wait(barrier, len(peers))
 
     zc = z * 2 + c
@@ -242,8 +244,14 @@
         sel = jnp.broadcast_to(target[:, 0:1], (2 * ROWS, depth)) == iota((2 * ROWS, depth), 1)
         sel = jnp.where(sel, 1.0, 0.0).astype(BF16)
         rows = pl.ds(pl.multiple_of(q * KQ, KQ), KQ) if h == 0 else pl.ds(0, 4 * KQ)
-        for lo, w in PIECES[h]:
-            snd[h][delta, :, lo : lo + w] = dot(sel, ev[rows, h * SPLIT + lo : h * SPLIT + lo + w]).astype(BF16)
+        for lo, w in PIECES:
+            snd[h][delta, :, lo : lo + w] = dot(sel, ev[rows, FIRST[h] + lo : FIRST[h] + lo + w]).astype(BF16)
+        if h == 0:
+            tail = dot(sel, ev[rows, DPAD - 128 : DPAD])
+            snd[h][delta, :, SPLIT : SPLIT + 128] = tail.astype(BF16)
+            for k in range(2):
+                upper, lower = (tail[k * ROWS + j * HALF : k * ROWS + j * HALF + HALF] for j in range(2))
+                tls[delta, k] = (upper + pltpu.roll(lower, 64, 1)).astype(BF16)
 
     def core_rows(cc):
         return pl.ds(pl.multiple_of(cc * ROWS, 16), ROWS)
@@ -251,21 +259,26 @@
     def piece(h, ref, row, n):
         if n == N:
             return ref.at[pl.ds(pl.multiple_of(row + MAIN, 16), LAST), :]
-        return ref.at[pl.ds(pl.multiple_of(row, 16), MAIN), pl.ds(*PIECES[h][n])]
+        return ref.at[pl.ds(pl.multiple_of(row, 16), MAIN), pl.ds(*PIECES[n])]
 
     def landing(h, slot, n):
-        return exl[h].at[slot] if n == N else ex[h].at[slot, :, pl.ds(*PIECES[h][n])]
+        return exl[h].at[slot] if n == N else ex[h].at[slot, :, pl.ds(*PIECES[n])]
 
     def landed(h, pair, n):
         return last_r.at[h] if n == N else exr.at[h, pair, n]
 
+    def leaving(h, n):
+        return (G_LS if n == N else G_EX) + h
+
     for h in range(2):
         gather(h, 2)
         for d in range(2):
+            if h == 0:
+                send(tls.at[2, d], trt.at[d], G_TL, tr_r.at[d], ex_dev[0](1 - 2 * d, c))
             for n in range(N + 1):
                 send(
                     piece(h, snd[h].at[2], d * ROWS, n), piece(h, tr[h].at[d], 0, n),
-                    G_EX + h, ex2_r.at[h, d, n], ex_dev[h](1 - 2 * d, c),
+                    leaving(h, n), ex2_r.at[h, d, n], ex_dev[h](1 - 2 * d, c),
                 )
 
     def gather_rest(o, _):
@@ -284,14 +297,18 @@
                     slot = 3 - d + 4 * far
                     send(
                         piece(h, snd[h].at[1 + 2 * d], cc * ROWS, n), landing(h, slot, n),
-                        G_EX + h, landed(h, 1 + 2 * far, n), ex_dev[h](1 - 2 * d, cc),
+                        leaving(h, n), landed(h, 1 + 2 * far, n), ex_dev[h](1 - 2 * d, cc),
                     )
+                    if h == 0 and n == 0:
+                        send(tls.at[1 + 2 * d, cc], ext.at[slot], G_TL, tail_r.at[1 + 2 * far], ex_dev[0](1 - 2 * d, cc))
 
     ex1_send(0, range(N))
+    send(tls.at[0, other], ext.at[1], G_TO, tail_r.at[0], at(cc=other))
+    ext[0] = tls[0, c]
     for h in range(2):
         for n in range(N + 1):
-            send(piece(h, snd[h].at[0], other * ROWS, n), landing(h, 1, n), G_OWN + h, landed(h, 0, n), at(cc=other))
-        ex[h][0] = snd[h][0, pl.ds(pl.multiple_of(c * ROWS, 16), MAIN), :]
+            send(piece(h, snd[h].at[0], other * ROWS, n), landing(h, 1, n), (G_OL if n == N else G_OWN) + h, landed(h, 0, n), at(cc=other))
+        ex[h][0] = snd[h][0, pl.ds(pl.multiple_of(c * ROWS, 16), MAIN), 0:SPLIT]
         exl[h][0] = snd[h][0, pl.ds(pl.multiple_of(c * ROWS + MAIN, 16), LAST), :]
 
     for h in range(2):
@@ -305,6 +322,7 @@
             rowsel[h, :, i * T : (i + 1) * T] = jnp.where(valid & (place < MAIN), slot * MAIN + place, -1).astype(F32)
             rowlast[h, i] = jnp.where(valid & (place >= MAIN), slot * LAST + place - MAIN, -1).astype(F32)
         got(og[h].at[0 : 2 * T, :], og_r.at[h, 2])
+    ogr[...] = pltpu.roll(og0[:, SPLIT : SPLIT + 128].astype(F32), 64, 1).astype(BF16)
     acc[...] = jnp.zeros_like(acc)
 
     def absorb(pair, mine):
@@ -313,14 +331,24 @@
                 if mine:
                     got(landing(h, 1, n), landed(h, 0, n))
                 else:
-                    got(ex[h].at[pl.ds(2 * pair, 2), :, pl.ds(*PIECES[h][n])], landed(h, pair, n))
-                lo, w = PIECES[h][n]
+                    got(ex[h].at[pl.ds(2 * pair, 2), :, pl.ds(*PIECES[n])], landed(h, pair, n))
+                lo, w = PIECES[n]
                 block = ex[h][pl.ds(2 * pair, 2), :, lo : lo + w].reshape(2 * MAIN, w)
                 part = dot(block, og[h][:, lo : lo + w], ((1,), (1,)))
                 if n == 0:
                     gbuf[h] = part
                 else:
                     gbuf[h] += part
+        if mine:
+            got(ext.at[1], tail_r.at[0])
+        else:
+            got(ext.at[pl.ds(2 * pair, 2)], tail_r.at[pair])
+        tail = ext[pl.ds(2 * pair, 2)].reshape(MAIN, 128)
+        for j, other_side in enumerate((og0[:, SPLIT : SPLIT + 128], ogr[...])):
+            part = dot(tail, other_side, ((1,), (1,)))
+            for slot in range(2):
+                where = slice(slot * MAIN + j * HALF, slot * MAIN + j * HALF + HALF)
+                gbuf[0, where, :] += part[slot * HALF : slot * HALF + HALF]
         rid = (iota((2 * MAIN, 128), 0) + pair * 2 * MAIN).astype(F32)
         for h in range(2):
             for lb in range(6):
@@ -338,9 +366,12 @@
                 got(piece(h, tr[h].at[d], 0, n), ex2_r.at[h, d, n])
                 send(
                     piece(h, tr[h].at[d], 0, n), landing(h, 4 + c, n),
-                    G_EX + h, landed(h, 2, n), ex_dev[h](1 - 2 * d, d),
+                    leaving(h, n), landed(h, 2, n), ex_dev[h](1 - 2 * d, d),
                 )
 
+    for d in range(2):
+        got(trt.at[d], tr_r.at[d])
+        send(trt.at[d], ext.at[4 + c], G_TL, tail_r.at[2], ex_dev[0](1 - 2 * d, d))
     for n in range(N):
         forward(n)
     ex1_send(1, range(N))
@@ -455,14 +486,16 @@
     small_o[4:8, :] = jnp.broadcast_to(loss, (4, OUT))
 
     for h in range(2):
-        drain(snd[h], G_EX + h)
-        drain(snd[h].at[0, 0:ROWS, :], G_OWN + h)
+        drain(ex[h], G_EX + h)
+        drain(exl[h], G_LS + h)
+        drain(ex[h].at[0], G_OWN + h)
+        drain(exl[h].at[0], G_OL + h)
         drain(og[h].at[0 : 3 * T, :], G_OG + h)
         drain(metar.at[h, 0:3], G_ME + h)
         drain(pdr.at[h, 0:3], G_PD + h)
     for ref, group in (
         (cntr.at[0, 0:7], G_C1), (cntr.at[0:3], G_C2), (psr1.at[0:7], G_P1), (psr2.at[0:3], G_P2), (xcr.at[0:3], G_XC), (xpr.at[0:3], G_XP),
-        (tokr.at[0:7], G_TK), (spr.at[0:7], G_SP), (selr.at[0:7], G_LG), (rsr.at[0:15], G_RS),
+        (tokr.at[0:7], G_TK), (spr.at[0:7], G_SP), (tls, G_TL), (tls.at[0, 0], G_TO), (selr.at[0:7], G_LG), (rsr.at[0:15], G_RS),
     ):
         drain(ref, group)
     got(rsr.at[0:15], rr.at[12])
@@ -493,7 +526,8 @@
         vm((K, T), I32), vm((4, ES, 8, D), BF16), vm((4 * KQ, DPAD), BF16), vm((D, E), BF16), vm((1, E), F32),
         vm((4, 2 * ROWS, WIDTH[0]), BF16), vm((4, 2 * ROWS, WIDTH[1]), BF16),
         vm((2, ROWS, WIDTH[0]), BF16), vm((2, ROWS, WIDTH[1]), BF16),
-        vm((8, MAIN, WIDTH[0]), BF16), vm((8, MAIN, WIDTH[1]), BF16), vm((8, LAST, WIDTH[0]), BF16), vm((8, LAST, WIDTH[1]), BF16),
+        vm((8, MAIN, SPLIT), BF16), vm((8, MAIN, SPLIT), BF16), vm((8, LAST, WIDTH[0]), BF16), vm((8, LAST, WIDTH[1]), BF16),
+        vm((4, 2, HALF, 128), BF16), vm((2, HALF, 128), BF16), vm((8, HALF, 128), BF16), vm((4 * T, 128), BF16),
         vm((8, T, BLK), BF16),
         vm((8, E), F32), vm((4, 8, 8, E), F32), vm((K, 256, E), BF16), vm((8, 256), F32), vm((2, 4, 8, 256), F32),
         vm((2, K, 4 * T), F32), vm((2, 4, K, T), F32), vm((2, K, 8, 4 * T), F32), vm((2, 2 * MAIN, 4 * T), F32), vm((2, 4, K, 256), F32), vm((2, 4, K, 256), F32),
@@ -501,7 +535,7 @@
         vm((8, E), F32), vm((4, 8, E), F32), vm((8, E), F32), vm((4, 8, E), F32),
         vm((E, T), F32), vm((E, T), F32), vm((K, T), F32), vm((2, 72, 256), F32), vm((8, 72, 256), F32),
         vm((K, 256), F32), vm((8, K, 256), F32), vm((16, 4, OUT), F32), vm((16, 4, OUT), F32), vm((T, E), BF16),
-        dma((9,)), dma((20,)), dma((13,)), dma((2, 3)), dma((2, 2, N + 1)), dma((2, 4, N)), dma((2,)), dma((8,)),
+        dma((9,)), dma((26,)), dma((13,)), dma((2, 3)), dma((2, 2, N + 1)), dma((2, 4, N)), dma((2,)), dma((2,)), dma((4,)), dma((8,)),
     ]
     hbm = pl.BlockSpec(memory_space=pltpu.HBM)
     in_vmem = pl.BlockSpec(memory_space=vm)

time: 72.6 us -> 71.5 us (0.985)
  Pallas kernels: 71.2 us -> 69.9 us
    pallas_call x1, Pallas kernels: 70.2 us -> 68.9 us  [on_device(): pl.pallas_call(kernel, out_shape=(vm((T, D), BF16), vm((8, OUT), F32)), i...]
where the time goes in v5:
time: 71.5 us; the launch traced here: 71.2 us
  Pallas kernels  69.9 us (98%)
  between operations  1.29 us (2%)
    pallas_call x1, Pallas kernels, on_device(): pl.pallas_call(kernel, out_shape=(vm((T, D), BF16), vm((8, OUT), F32)), i...  68.9 us

profile of v5, /device:TPU:1, one launch (start us, length us, event | category | flops | bytes accessed | tf_op | source)
XLA Modules:
  0.0 71.2 jit_solution(6494977924352305264)
XLA Ops:
  1.3 68.9 %router.1 = (bf16[192,2880]{1,0:T(8,128)(2,1)S(1)}, f32[8,768]{1,0:T(8,128)S(1)}) custom-call(bf16[192,2880]{1,0:T(8,128)(2,1)} %tok_h.1, bf16[192,2880]{1,0:T(8,128)(2,1)} %og_h.1, s32[4,192]{1,0:T(4,128)} %bitcast.9, bf16[36,32,2880]{2,1,0:T(8,128)(2,1)} %bitcast.8, bf16[2880,128]{1,0:T(8,128)(2,1)} %w_h.1, f32[1,128]{1,0:T(1,128)} %bitcast.10, ...), custom_call_target="tpu_custom_call" | custom-call | tf_op jit(solution)/shard_map/router/pallas_call | solution.py:542
  70.2 1.0 %finish.1 = (bf16[192,2880]{1,0:T(8,128)(2,1)}, f32[4,720]{1,0:T(4,128)}, f32[1]{0:T(128)}) custom-call(bf16[192,2880]{1,0:T(8,128)(2,1)S(1)} %get-tuple-element.8.tg_ref, f32[8,768]{1,0:T(8,128)S(1)} %get-tuple-element.9.small_ref), custom_call_target="tpu_custom_call" | custom-call | tf_op jit(solution)/shard_map/finish/pallas_call | solution.py:557

commit v6 on v5

--- a/solution.py
+++ b/solution.py
@@ -22,15 +22,14 @@
 MAIN, LAST = 96, 16
 ES = 4 * CAP
 KQ = ES * 8
-PIECES = ((0, 640), (640, 512), (1152, 256))
+PIECES = ((0, 640), (640, 640), (1280, 128))
 N = 3
 HALF = MAIN // 2
 BLK = 896
 OUT = 768
 TOTAL = 24576
-G_EX, G_OWN, G_OG, G_ME, G_PD = 0, 2, 4, 6, 8
-G_C1, G_C2, G_P1, G_P2, G_XC, G_XP, G_TK, G_SP, G_LG, G_RS = range(10, 20)
-G_TL, G_TO, G_LS, G_OL = 20, 21, 22, 24
+G_EX, G_OWN, G_OG, G_LS, G_OL = 0, 2, 4, 6, 8
+G_SMALL, G_TK, G_SP, G_RS, G_TL, G_TO = range(10, 16)
 
 
 def dot(a, b, dims=((1,), (0,)), **kw):
@@ -82,8 +81,12 @@
         pltpu.make_async_copy(tok_h, tokraw, loc.at[2]),
         pltpu.make_async_copy(w_h, wv, loc.at[3]),
         pltpu.make_async_copy(b_h, bv, loc.at[4]),
-    ] + [pltpu.make_async_copy(ex_h.at[:, q * 8 : q * 8 + 8, :], ev3.at[q], loc.at[5 + q]) for q in range(4)]
-    for l in loads:
+    ] + [pltpu.make_async_copy(ex_h.at[:, q * 8 : q * 8 + 8, :], ev3.at[q], loc.at[5]) for q in range(4)]
+    loads[0].start()
+    for n in range(4):
+        rows = pl.ds(48 * n, 48)
+        pltpu.make_async_copy(og_h.at[rows, :], ogfull.at[rows, :], loc.at[1]).start()
+    for l in loads[2:]:
         l.start()
     peers = [at(dy=a, dz=b) for a in range(4) for b in range(4) if a or b]
     peers += [at(dy=a, cc=other) for a in (1, 2, 3)] + [at(dz=a, cc=other) for a in (1, 2, 3)]
@@ -130,10 +133,10 @@
     zpeers = [(b, k) for b in (1, 2, 3) for k in (0, 1)] + [(0, 1)]
     zdev = lambda b, k: at(dz=b, cc=lax.rem(c + k, 2))
     for n, (b, k) in enumerate(zpeers):
-        send(cntsnd, cntr.at[y, zc], G_C1, rr.at[0], zdev(b, k))
+        send(cntsnd, cntr.at[y, zc], G_SMALL, rr.at[0], zdev(b, k))
     for h in range(2):
         for s in (1, 2, 3):
-            send(meta, metar.at[h, po[h]], G_ME + h, rr.at[2 + h], og_dev[h](s))
+            send(meta, metar.at[h, po[h]], G_SMALL, rr.at[2 + h], og_dev[h](s))
 
     def og_rows(pos, second):
         return pl.ds(pl.multiple_of(pos * T + second * 96, 32), 96)
@@ -148,7 +151,7 @@
 
     got(cntr.at[0, 0:7], rr.at[0])
     for s in (1, 2, 3):
-        send(cntr.at[y], cntr.at[y], G_C2, rr.at[1], at(dy=s))
+        send(cntr.at[y], cntr.at[y], G_SMALL, rr.at[1], at(dy=s))
     for h in range(2):
         for d in range(2):
             og_send(h, d, 1)
@@ -185,11 +188,10 @@
     prow = jnp.sum(jnp.where(diag, pcol, 0.0), axis=0, keepdims=True)
     psb[...] = jnp.broadcast_to(prow, (8, E))
     for n, (b, k) in enumerate(zpeers):
-        send(psb, psr1.at[zc], G_P1, rr.at[5], zdev(b, k))
+        send(psb, psr1.at[zc], G_SMALL, rr.at[5], zdev(b, k))
     psr1[zc] = psb[...]
 
-    for q in range(4):
-        loads[5 + q].wait()
+    pltpu.make_async_copy(ev3, ev3, loc.at[5]).wait()
     ev[:, DPAD - 128 : DPAD] = jnp.zeros((4 * KQ, 128), BF16)
 
     def flatten(n, _):
@@ -215,7 +217,7 @@
     xcs[...] = plane
     xcr[x] = plane
     for a in (1, 2, 3):
-        send(xcs, xcr.at[x], G_XC, rr.at[7], at(dx=a))
+        send(xcs, xcr.at[x], G_SMALL, rr.at[7], at(dx=a))
     first = (y * 8 + z * 2 + c) * 4
     cb = counts.reshape(256, E).astype(BF16)
     for k in range(K):
@@ -265,7 +267,7 @@
         return exl[h].at[slot] if n == N else ex[h].at[slot, :, pl.ds(*PIECES[n])]
 
     def landed(h, pair, n):
-        return last_r.at[h] if n == N else exr.at[h, pair, n]
+        return last_r.at[h] if n == N else exr.at[pair, n]
 
     def leaving(h, n):
         return (G_LS if n == N else G_EX) + h
@@ -327,11 +329,11 @@
 
     def absorb(pair, mine):
         for n in range(N):
+            if mine:
+                got(ex[0].at[0:2, :, pl.ds(*PIECES[n])], exr.at[0, n])
+            else:
+                got(ex[0].at[0:4, :, pl.ds(*PIECES[n])], exr.at[pair, n])
             for h in range(2):
-                if mine:
-                    got(landing(h, 1, n), landed(h, 0, n))
-                else:
-                    got(ex[h].at[pl.ds(2 * pair, 2), :, pl.ds(*PIECES[n])], landed(h, pair, n))
                 lo, w = PIECES[n]
                 block = ex[h][pl.ds(2 * pair, 2), :, lo : lo + w].reshape(2 * MAIN, w)
                 part = dot(block, og[h][:, lo : lo + w], ((1,), (1,)))
@@ -339,16 +341,17 @@
                     gbuf[h] = part
                 else:
                     gbuf[h] += part
-        if mine:
-            got(ext.at[1], tail_r.at[0])
-        else:
-            got(ext.at[pl.ds(2 * pair, 2)], tail_r.at[pair])
-        tail = ext[pl.ds(2 * pair, 2)].reshape(MAIN, 128)
-        for j, other_side in enumerate((og0[:, SPLIT : SPLIT + 128], ogr[...])):
-            part = dot(tail, other_side, ((1,), (1,)))
-            for slot in range(2):
-                where = slice(slot * MAIN + j * HALF, slot * MAIN + j * HALF + HALF)
-                gbuf[0, where, :] += part[slot * HALF : slot * HALF + HALF]
+            if n == 0:
+                if mine:
+                    got(ext.at[1], tail_r.at[0])
+                else:
+                    got(ext.at[pl.ds(2 * pair, 2)], tail_r.at[pair])
+                tail = ext[pl.ds(2 * pair, 2)].reshape(MAIN, 128)
+                for j, other_side in enumerate((og0[:, SPLIT : SPLIT + 128], ogr[...])):
+                    part = dot(tail, other_side, ((1,), (1,)))
+                    for slot in range(2):
+                        where = slice(slot * MAIN + j * HALF, slot * MAIN + j * HALF + HALF)
+                        gbuf[0, where, :] += part[slot * HALF : slot * HALF + HALF]
         rid = (iota((2 * MAIN, 128), 0) + pair * 2 * MAIN).astype(F32)
         for h in range(2):
             for lb in range(6):
@@ -383,7 +386,7 @@
     psb2[...] = jnp.sum(psr1[...], axis=0)
     psr2[y] = psb2[...]
     for s in (1, 2, 3):
-        send(psb2, psr2.at[y], G_P2, rr.at[6], at(dy=s))
+        send(psb2, psr2.at[y], G_SMALL, rr.at[6], at(dy=s))
 
     got(xcr.at[0:3], rr.at[7])
     cnt_row = jnp.sum(xcr[...], axis=0)[0:1, :]
@@ -415,13 +418,8 @@
             for k in range(K):
                 pds[h, i, k : k + 1, 0:T] = jnp.sum(acc[h, k, :, i * T : (i + 1) * T], axis=0, keepdims=True)
         for s in (1, 2, 3):
-            send(pds.at[h, m4(po[h] + s)], pdr.at[h, po[h]], G_PD + h, rr.at[10 + h], og_dev[h](s))
+            send(pds.at[h, m4(po[h] + s)], pdr.at[h, po[h]], G_SMALL, rr.at[10 + h], og_dev[h](s))
         pdr[h, po[h]] = pds[h, po[h]]
-    got(psr2.at[0:3], rr.at[6])
-    xps[...] = jnp.sum(psr2[...], axis=0)
-    xpr[x] = xps[...]
-    for a in (1, 2, 3):
-        send(xps, xpr.at[x], G_XP, rr.at[8], at(dx=a))
     late = [jnp.zeros((1, T), F32)] * K
     rid = iota((8 * LAST, T), 0).astype(F32)
     for h in range(2):
@@ -445,12 +443,17 @@
         selb[k : k + 1, 0:T] = mix[k] * (dots[k] - mean)
     selb[:, T:256] = jnp.zeros((K, 256 - T), F32)
     for n, (a, k) in enumerate(xpeers):
-        send(selb, selr.at[xc], G_LG, lg_r.at[xc], xdev(a, k))
+        send(selb, selr.at[xc], G_SMALL, lg_r.at[xc], xdev(a, k))
 
     lg = jnp.zeros((E, T), F32)
     for k in range(K):
         lg += jnp.where(idxv[k : k + 1, :] == ie, selb[k : k + 1, 0:T], 0.0)
     lgv[...] = jnp.transpose(lt[...] + lg).astype(BF16)
+    got(psr2.at[0:3], rr.at[6])
+    xps[...] = jnp.sum(psr2[...], axis=0)
+    xpr[x] = xps[...]
+    for a in (1, 2, 3):
+        send(xps, xpr.at[x], G_SMALL, rr.at[8], at(dx=a))
     got(tokr.at[0:7], rr.at[4])
     got(spr.at[0:7], rr.at[9])
 
@@ -491,11 +494,9 @@
         drain(ex[h].at[0], G_OWN + h)
         drain(exl[h].at[0], G_OL + h)
         drain(og[h].at[0 : 3 * T, :], G_OG + h)
-        drain(metar.at[h, 0:3], G_ME + h)
-        drain(pdr.at[h, 0:3], G_PD + h)
     for ref, group in (
-        (cntr.at[0, 0:7], G_C1), (cntr.at[0:3], G_C2), (psr1.at[0:7], G_P1), (psr2.at[0:3], G_P2), (xcr.at[0:3], G_XC), (xpr.at[0:3], G_XP),
-        (tokr.at[0:7], G_TK), (spr.at[0:7], G_SP), (tls, G_TL), (tls.at[0, 0], G_TO), (selr.at[0:7], G_LG), (rsr.at[0:15], G_RS),
+        (spr.at[0:4], G_SMALL),
+        (tokr.at[0:7], G_TK), (spr.at[0:7], G_SP), (tls, G_TL), (tls.at[0, 0], G_TO), (rsr.at[0:15], G_RS),
     ):
         drain(ref, group)
     got(rsr.at[0:15], rr.at[12])
@@ -504,8 +505,9 @@
 
 
 def finish(tg_ref, small_ref, tg_o, wt_o, loss_o, wtv, lossv, sem):
-    tg_out = pltpu.make_async_copy(tg_ref, tg_o, sem.at[0])
-    tg_out.start()
+    tg_out = [pltpu.make_async_copy(tg_ref.at[48 * n : 48 * n + 48], tg_o.at[48 * n : 48 * n + 48], sem.at[3 + n]) for n in range(4)]
+    for t in tg_out:
+        t.start()
     wtv[...] = small_ref[0:4, 0:720]
     wt_out = pltpu.make_async_copy(wtv, wt_o, sem.at[1])
     wt_out.start()
@@ -513,7 +515,8 @@
     loss_out = pltpu.make_async_copy(lossv, loss_o, sem.at[2])
     loss_out.start()
     loss_out.wait()
-    tg_out.wait()
+    for t in tg_out:
+        t.wait()
     wt_out.wait()
 
 
@@ -535,7 +538,7 @@
         vm((8, E), F32), vm((4, 8, E), F32), vm((8, E), F32), vm((4, 8, E), F32),
         vm((E, T), F32), vm((E, T), F32), vm((K, T), F32), vm((2, 72, 256), F32), vm((8, 72, 256), F32),
         vm((K, 256), F32), vm((8, K, 256), F32), vm((16, 4, OUT), F32), vm((16, 4, OUT), F32), vm((T, E), BF16),
-        dma((9,)), dma((26,)), dma((13,)), dma((2, 3)), dma((2, 2, N + 1)), dma((2, 4, N)), dma((2,)), dma((2,)), dma((4,)), dma((8,)),
+        dma((6,)), dma((16,)), dma((13,)), dma((2, 3)), dma((2, 2, N + 1)), dma((4, N)), dma((2,)), dma((2,)), dma((4,)), dma((8,)),
     ]
     hbm = pl.BlockSpec(memory_space=pltpu.HBM)
     in_vmem = pl.BlockSpec(memory_space=vm)
@@ -563,7 +566,7 @@
         ),
         in_specs=[in_vmem] * 2,
         out_specs=(hbm, hbm, hbm),
-        scratch_shapes=[vm((4, 720), F32), pltpu.SMEM((1,), F32), dma((3,))],
+        scratch_shapes=[vm((4, 720), F32), pltpu.SMEM((1,), F32), dma((7,))],
         name="finish",
     )(*(pltpu.with_memory_space_constraint(a, vm) for a in (token_grad, small)))
     return token_grad, weight_grad.T, loss

time: 71.5 us -> 71 us (level)
  no operation moved by 1% of the time
where the time goes in v6:
time: 71 us; the launch traced here: 70.7 us
  Pallas kernels  69.5 us (98%)
  between operations  1.29 us (2%)
    pallas_call x1, Pallas kernels, on_device(): pl.pallas_call(kernel, out_shape=(vm((T, D), BF16), vm((8, OUT), F32)), i...  68.4 us

profile of v6, /device:TPU:1, one launch (start us, length us, event | category | flops | bytes accessed | tf_op | source)
XLA Modules:
  0.0 70.7 jit_solution(16341636979091636446)
XLA Ops:
  1.3 68.4 %router.1 = (bf16[192,2880]{1,0:T(8,128)(2,1)S(1)}, f32[8,768]{1,0:T(8,128)S(1)}) custom-call(bf16[192,2880]{1,0:T(8,128)(2,1)} %tok_h.1, bf16[192,2880]{1,0:T(8,128)(2,1)} %og_h.1, s32[4,192]{1,0:T(4,128)} %bitcast.9, bf16[36,32,2880]{2,1,0:T(8,128)(2,1)} %bitcast.8, bf16[2880,128]{1,0:T(8,128)(2,1)} %w_h.1, f32[1,128]{1,0:T(1,128)} %bitcast.10, ...), custom_call_target="tpu_custom_call" | custom-call | tf_op jit(solution)/shard_map/router/pallas_call | solution.py:545
  69.7 1.1 %finish.1 = (bf16[192,2880]{1,0:T(8,128)(2,1)}, f32[4,720]{1,0:T(4,128)}, f32[1]{0:T(128)}) custom-call(bf16[192,2880]{1,0:T(8,128)(2,1)S(1)} %get-tuple-element.8.tg_ref, f32[8,768]{1,0:T(8,128)S(1)} %get-tuple-element.9.small_ref), custom_call_target="tpu_custom_call" | custom-call | tf_op jit(solution)/shard_map/finish/pallas_call | solution.py:560

commit v7 on v6

--- a/solution.py
+++ b/solution.py
@@ -88,8 +88,7 @@
         pltpu.make_async_copy(og_h.at[rows, :], ogfull.at[rows, :], loc.at[1]).start()
     for l in loads[2:]:
         l.start()
-    peers = [at(dy=a, dz=b) for a in range(4) for b in range(4) if a or b]
-    peers += [at(dy=a, cc=other) for a in (1, 2, 3)] + [at(dz=a, cc=other) for a in (1, 2, 3)]
+    peers = [at(dy=a) for a in (1, 2, 3)] + [at(dz=a, cc=k) for a in (1, 2, 3) for k in (c, other)]
     peers += [at(cc=other)] + [at(dx=a, cc=k) for a in (1, 2, 3) for k in (c, other)]
     barrier = pltpu.get_barrier_semaphore()
     for p in peers:

time: 71 us -> 70.3 us (level)
  no operation moved by 1% of the time
where the time goes in v7:
time: 70.3 us; the launch traced here: 70.2 us
  Pallas kernels  68.9 us (98%)
  between operations  1.29 us (2%)
    pallas_call x1, Pallas kernels, on_device(): pl.pallas_call(kernel, out_shape=(vm((T, D), BF16), vm((8, OUT), F32)), i...  67.9 us

profile of v7, /device:TPU:1, one launch (start us, length us, event | category | flops | bytes accessed | tf_op | source)
XLA Modules:
  0.0 70.2 jit_solution(8186707816592108942)
XLA Ops:
  1.3 67.9 %router.1 = (bf16[192,2880]{1,0:T(8,128)(2,1)S(1)}, f32[8,768]{1,0:T(8,128)S(1)}) custom-call(bf16[192,2880]{1,0:T(8,128)(2,1)} %tok_h.1, bf16[192,2880]{1,0:T(8,128)(2,1)} %og_h.1, s32[4,192]{1,0:T(4,128)} %bitcast.9, bf16[36,32,2880]{2,1,0:T(8,128)(2,1)} %bitcast.8, bf16[2880,128]{1,0:T(8,128)(2,1)} %w_h.1, f32[1,128]{1,0:T(1,128)} %bitcast.10, ...), custom_call_target="tpu_custom_call" | custom-call | tf_op jit(solution)/shard_map/router/pallas_call | solution.py:544
  69.2 1.1 %finish.1 = (bf16[192,2880]{1,0:T(8,128)(2,1)}, f32[4,720]{1,0:T(4,128)}, f32[1]{0:T(128)}) custom-call(bf16[192,2880]{1,0:T(8,128)(2,1)S(1)} %get-tuple-element.8.tg_ref, f32[8,768]{1,0:T(8,128)S(1)} %get-tuple-element.9.small_ref), custom_call_target="tpu_custom_call" | custom-call | tf_op jit(solution)/shard_map/finish/pallas_call | solution.py:559
